TPU v7x, 32 devices: a whole 2x2x4 slice. The times are simulated.
32 devices in a mesh: rows: 8 (over y, x, core), rhs: 4 (over z).
Axes of the slice: x: 2, y: 2, z: 4, core: 2. Of those that a mesh axis runs over, the one named last changes fastest.
Arguments:
- band_blocks: float32 [64, 256, 1280], P('rows'), may hold values from -12 to 12
- precond_blocks: float32 [64, 256, 256], P('rows'), may hold values from -2 to 2
- right_side: float32 [16384, 2048], P('rows', 'rhs'), may hold values from -80 to 80
Outputs:
- solution: float32 [16384, 2048], P('rows', 'rhs')
- scaled_residual: float32 [16384, 2048], P('rows', 'rhs')
- rms_history: float32 [3, 2048], P(None, 'rhs')
- overall_rms: float32 [], replicated
All inputs are finite; a program needn't handle non-finite values.
Results may differ from a plain program's by a relative error of at most 0.0003.
Values sent between devices are 32-bit elements; how exact they have to be, the bound alone decides.
No kernel may reach another device: no remote copies, remote signals or barrier semaphores. Data moves between devices by JAX's collectives and lax.ppermute only.
A program may use at most 128 MiB of HBM per device.

v0:
```python
import jax
import jax.numpy as jnp
from jax import lax
from jax.sharding import PartitionSpec as P

ITERS = 2


def extended(block, sides, width):
    for axis, dim in sides:
        count = lax.axis_size(axis)
        forward = [(i, i + 1) for i in range(count - 1)]
        backward = [(target, source) for source, target in forward]
        low = lax.ppermute(
            lax.slice_in_dim(block, block.shape[dim] - width, None, axis=dim), axis, forward
        )
        high = lax.ppermute(lax.slice_in_dim(block, 0, width, axis=dim), axis, backward)
        block = jnp.concatenate([low, block, high], axis=dim)
    return block


def band_times(band_blocks, padded):
    block_rows = band_blocks.shape[1]
    pieces = []
    for number in range(band_blocks.shape[0]):
        window = padded[number * block_rows : (number + 5) * block_rows]
        pieces.append(
            jnp.dot(
                band_blocks[number],
                window,
                precision=lax.Precision.HIGHEST,
                preferred_element_type=jnp.float32,
            )
        )
    return jnp.concatenate(pieces, axis=0)


def precondition(precond_blocks, operand):
    shaped = operand.reshape(precond_blocks.shape[0], precond_blocks.shape[1], operand.shape[1])
    return jnp.einsum(
        "jab,jbc->jac", precond_blocks, shaped, precision=lax.Precision.HIGHEST
    ).reshape(operand.shape)


def column_squares(residual):
    partial_value = jnp.sum(residual * residual, axis=0)
    return lax.psum(partial_value, "rows")


def shards(band_blocks, precond_blocks, right_side):
    block_rows = band_blocks.shape[1]
    solution = precondition(precond_blocks, right_side)
    sums = []
    residual = right_side
    for sweep in range(ITERS + 1):
        rimmed = extended(solution, (("rows", 0),), 2 * block_rows)
        residual = right_side - band_times(band_blocks, rimmed)
        sums.append(column_squares(residual))
        if sweep < ITERS:
            solution = solution + precondition(precond_blocks, residual)
    stacked = jnp.stack(sums)
    total_rows = lax.axis_size("rows") * right_side.shape[0]
    all_columns = lax.axis_size("rhs") * right_side.shape[1]
    history = jnp.sqrt(stacked / total_rows + 1e-06)
    scaled_residual = residual / history[ITERS][None, :]
    grand_total = lax.psum(jnp.sum(stacked[ITERS]), "rhs")
    overall_rms = jnp.sqrt(grand_total / (total_rows * all_columns) + 1e-06)
    return (solution, scaled_residual, history, overall_rms)


def solution(mesh):
    in_specs = (P("rows", None, None), P("rows", None, None), P("rows", "rhs"))
    out_specs = (P("rows", "rhs"), P("rows", "rhs"), P(None, "rhs"), P())
    return jax.shard_map(shards, mesh=mesh, in_specs=in_specs, out_specs=out_specs, check_vma=False)
```

profile of v0, /device:TPU:4, one launch (start us, length us, event | category | flops | bytes accessed | tf_op | source)
XLA Modules:
  0.0 222.5 jit_solution(1570749463246648001)
XLA Ops:
  2.2 5.5 %fusion.316 = f32[8,256,512]{2,1,0:T(8,128)S(1)} fusion(f32[8,256,256]{2,1,0:T(8,128)S(1)} %copy-done, f32[8,256,512]{2,1,0:T(8,128)} %bitcast.289), kind=kOutput, calls=%fused_computation.183 | convolution fusion | flops 3221225472 | bytes 10485760 | tf_op jit(solution)/shard_map/jab,jbc->jac/dot_general | solution.py:40
  11.1 4.7 %collective-permute-start.1 = (f32[512,512]{1,0:T(8,128)}, f32[512,512]{1,0:T(8,128)}, u32[]{:S(2)}, u32[]{:S(2)}) collective-permute-start(f32[512,512]{1,0:T(8,128)} %bitcast.19), channel_id=1, source_target_pairs={{4,0},{8,4},{12,8},{16,12},{20,16},{24,20},{28,24},{5,1},{9,5},{13... | collective-permute-start | bytes 3145736 | tf_op jit(solution)/shard_map/ppermute | solution.py:17
  15.9 3.0 %fusion.315 = (f32[5,256,512]{2,1,0:T(8,128)S(1)}, f32[5,256,512]{2,1,0:T(8,128)S(1)}, f32[5,256,512]{2,1,0:T(8,128)S(1)}, f32[5,256,512]{2,1,0:T(8,128)}) fusion(f32[8,256,512]{2,1,0:T(8,128)S(1)} %fusion.316), kind=kLoop, calls=%fused_computation.182 | loop fusion | bytes 20971520 | tf_op jit(solution)/shard_map/slice | solution.py:26
  18.9 16.1 %collective-permute-done = f32[512,512]{1,0:T(8,128)} collective-permute-done((f32[512,512]{1,0:T(8,128)}, f32[512,512]{1,0:T(8,128)}, u32[]{:S(2)}, u32[]{:S(2)}) %collective-permute-start) | collective-permute-done | bytes 1048608 | tf_op jit(solution)/shard_map/ppermute | solution.py:14
  35.0 5.0 %fusion.219 = f32[2048,512]{1,0:T(8,128)} fusion(f32[512,512]{1,0:T(8,128)} %collective-permute-done, f32[2048,512]{1,0:T(8,128)S(1)} %bitcast.281, f32[8,256,1280]{2,1,0:T(8,128)} %param.3), kind=kOutput, calls=%fused_computation.129 | convolution fusion | flops 2013921280 | bytes 7077888 | tf_op jit(solution)/shard_map/dot_general | solution.py:28
  40.1 4.9 %fusion.181 = f32[2048,512]{1,0:T(8,128)} fusion(f32[2048,512]{1,0:T(8,128)} %fusion.219, f32[2048,512]{1,0:T(8,128)S(1)} %bitcast.282, f32[512,512]{1,0:T(8,128)} %collective-permute-done, f32[8,256,1280]{2,1,0:T(8,128)} %param.3), kind=kOutput, calls=%fused_computation.117 | convolution fusion | flops 2013921280 | bytes 7077888 | tf_op jit(solution)/shard_map/dot_general | solution.py:28
  44.9 4.7 %fusion.77 = f32[2048,512]{1,0:T(8,128)} fusion(f32[2048,512]{1,0:T(8,128)} %fusion.181, f32[1280,512]{1,0:T(8,128)S(1)} %bitcast.295, f32[8,256,1280]{2,1,0:T(8,128)} %param.3), kind=kOutput, calls=%fused_computation.93 | convolution fusion | flops 2013265920 | bytes 4456448 | tf_op jit(solution)/shard_map/dot_general | solution.py:28
  49.7 4.6 %fusion.83 = f32[2048,512]{1,0:T(8,128)} fusion(f32[2048,512]{1,0:T(8,128)} %fusion.77, f32[1280,512]{1,0:T(8,128)S(1)} %bitcast.294, f32[8,256,1280]{2,1,0:T(8,128)} %param.3), kind=kOutput, calls=%fused_computation.95 | convolution fusion | flops 2013265920 | bytes 4456448 | tf_op jit(solution)/shard_map/dot_general | solution.py:28
  54.3 3.7 %fusion.89 = f32[2048,512]{1,0:T(8,128)} fusion(f32[2048,512]{1,0:T(8,128)} %fusion.83, f32[1280,512]{1,0:T(8,128)S(1)} %bitcast.293, f32[8,256,1280]{2,1,0:T(8,128)S(1)} %bitcast.286), kind=kOutput, calls=%fused_computation.97 | convolution fusion | flops 2013265920 | bytes 4456448 | tf_op jit(solution)/shard_map/dot_general | solution.py:28
  58.0 3.3 %fusion.95 = f32[2048,512]{1,0:T(8,128)} fusion(f32[2048,512]{1,0:T(8,128)} %fusion.89, f32[1280,512]{1,0:T(8,128)S(1)} %bitcast.292, f32[8,256,1280]{2,1,0:T(8,128)S(1)} %bitcast.286), kind=kOutput, calls=%fused_computation.99 | convolution fusion | flops 2013265920 | bytes 4456448 | tf_op jit(solution)/shard_map/dot_general | solution.py:28
  61.3 4.4 %fusion.229 = f32[2048,512]{1,0:T(8,128)} fusion(f32[2048,512]{1,0:T(8,128)} %fusion.95, f32[2048,512]{1,0:T(8,128)S(1)} %bitcast.283, f32[512,512]{1,0:T(8,128)} %collective-permute-done.1, f32[8,256,1280]{2,1,0:T(8,128)S(1)} %bitcast.286), kind=kOutput, calls=%fused_computation.131 | convolution fusion | flops 2013921280 | bytes 7077888 | tf_op jit(solution)/shard_map/dot_general | solution.py:28
  65.7 4.7 %fusion.187 = f32[2048,512]{1,0:T(8,128)} fusion(f32[2048,512]{1,0:T(8,128)} %fusion.229, f32[512,512]{1,0:T(8,128)} %collective-permute-done.1, f32[2048,512]{1,0:T(8,128)S(1)} %bitcast.284, f32[8,256,1280]{2,1,0:T(8,128)S(1)} %bitcast.286), kind=kOutput, calls=%fused_computation.119 | convolution fusion | flops 2013921280 | bytes 7077888 | tf_op jit(solution)/shard_map/dot_general | solution.py:28
  70.4 3.0 %multiply_reduce_fusion.2 = (f32[512]{0:T(512)S(1)}, f32[2048,512]{1,0:T(8,128)S(1)}) fusion(f32[2048,512]{1,0:T(8,128)S(1)} %copy-done.2, f32[2048,512]{1,0:T(8,128)} %fusion.187), kind=kLoop, calls=%fused_computation.16 | loop fusion | flops 3145216 | bytes 12584960 | tf_op jit(solution)/shard_map/reduce_sum | solution.py:46
  73.4 5.3 %fusion.317 = f32[8,512,256]{1,2,0:T(8,128)} fusion(f32[8,256,512]{2,1,0:T(8,128)S(1)} %bitcast.290, f32[8,256,256]{2,1,0:T(8,128)S(1)} %copy-done), kind=kOutput, calls=%fused_computation.184 | convolution fusion | flops 3221225472 | bytes 10485760 | tf_op jit(solution)/shard_map/jab,jbc->jac/dot_general | solution.py:40
  83.6 4.7 %collective-permute-start.3 = (f32[512,512]{1,0:T(8,128)S(1)}, f32[512,512]{1,0:T(8,128)S(1)}, u32[]{:S(2)}, u32[]{:S(2)}) collective-permute-start(f32[512,512]{1,0:T(8,128)S(1)} %get-tuple-element.15), channel_id=1, source_target_pairs={{4,0},{8,4},{12,8},{16,12},{20,16},{24,20},{28,24},{5,1},{9,5},{13... | collective-permute-start | bytes 3145736 | tf_op jit(solution)/shard_map/ppermute | solution.py:17
  88.3 20.8 %collective-permute-done.2 = f32[512,512]{1,0:T(8,128)S(1)} collective-permute-done((f32[512,512]{1,0:T(8,128)S(1)}, f32[512,512]{1,0:T(8,128)S(1)}, u32[]{:S(2)}, u32[]{:S(2)}) %collective-permute-start.2) | collective-permute-done | bytes 1048608 | tf_op jit(solution)/shard_map/ppermute | solution.py:14
  130.7 5.3 %fusion.318 = f32[8,512,256]{1,2,0:T(8,128)} fusion(f32[8,256,512]{2,1,0:T(8,128)S(1)} %bitcast.291, f32[8,256,256]{2,1,0:T(8,128)S(1)} %copy-done), kind=kOutput, calls=%fused_computation.185 | convolution fusion | flops 3221225472 | bytes 10485760 | tf_op jit(solution)/shard_map/jab,jbc->jac/dot_general | solution.py:40
  136.0 3.4 %bitcast_add_fusion = f32[2048,512]{1,0:T(8,128)S(1)} fusion(f32[2048,512]{1,0:T(8,128)S(1)} %bitcast_add_fusion.1, f32[8,512,256]{1,2,0:T(8,128)} %fusion.318), kind=kLoop, calls=%fused_computation.12 | loop fusion | flops 1048576 | bytes 12582912 | tf_op jit(solution)/shard_map/add | solution.py:60
  141.5 4.7 %collective-permute-start.5 = (f32[512,512]{1,0:T(8,128)S(1)}, f32[512,512]{1,0:T(8,128)S(1)}, u32[]{:S(2)}, u32[]{:S(2)}) collective-permute-start(f32[512,512]{1,0:T(8,128)S(1)} %get-tuple-element.13), channel_id=1, source_target_pairs={{4,0},{8,4},{12,8},{16,12},{20,16},{24,20},{28,24},{5,1},{9,5},{13... | collective-permute-start | bytes 3145736 | tf_op jit(solution)/shard_map/ppermute | solution.py:17
  146.2 20.8 %collective-permute-done.4 = f32[512,512]{1,0:T(8,128)S(1)} collective-permute-done((f32[512,512]{1,0:T(8,128)S(1)}, f32[512,512]{1,0:T(8,128)S(1)}, u32[]{:S(2)}, u32[]{:S(2)}) %collective-permute-start.4) | collective-permute-done | bytes 1048608 | tf_op jit(solution)/shard_map/ppermute | solution.py:14
  187.5 2.9 %multiply_reduce_fusion = (f32[512]{0:T(512)S(1)}, f32[2048,512]{1,0:T(8,128)}) fusion(f32[2048,512]{1,0:T(8,128)S(1)} %copy-done.2, f32[2048,512]{1,0:T(8,128)S(1)} %fusion.211), kind=kLoop, calls=%fused_computation.14 | loop fusion | flops 3145216 | bytes 12584960 | tf_op jit(solution)/shard_map/reduce_sum | solution.py:46
  190.4 12.1 %all-reduce = (f32[512]{0:T(512)S(1)}, f32[1,512]{1,0:T(1,128)S(1)}, f32[1,512]{1,0:T(1,128)S(1)}) all-reduce(f32[512]{0:T(512)S(1)} %get-tuple-element.11, f32[1,512]{1,0:T(1,128)S(1)} %bitcast.299, f32[1,512]{1,0:T(1,128)S(1)} %bitcast.298), channel_id=1, replica_groups=mesh['rows'=8,'rhs'=4] {'rows'}, use_global_device_ids=true, to_apply=%region_5.0 | all-reduce | flops 1536 | bytes 12288 | tf_op jit(solution)/shard_map/psum | solution.py:47
  203.1 12.6 %psum.31 = f32[]{:T(128)} all-reduce(f32[]{:T(128)} %reduce_sum.39), channel_id=1, replica_groups=mesh['rows'=8,'rhs'=4] {'rhs'}, use_global_device_ids=true, to_apply=%region_7.0 | all-reduce | flops 1 | bytes 8 | tf_op jit(solution)/shard_map/psum | solution.py:66
  216.4 4.8 %broadcast_divide_fusion = f32[2048,512]{1,0:T(8,128)} fusion(f32[2048,512]{1,0:T(8,128)} %get-tuple-element.12, f32[512]{0:T(512)S(1)} %bitcast.296), kind=kLoop, calls=%fused_computation.63 | loop fusion | flops 1048576 | bytes 8390656 | tf_op jit(solution)/shard_map/div | solution.py:65
  (54 shorter events, 54.3 us)
Async XLA Ops:
  0.6 1.6 copy-start
  9.2 25.8 %collective-permute-start = (f32[512,512]{1,0:T(8,128)}, f32[512,512]{1,0:T(8,128)}, u32[]{:S(2)}, u32[]{:S(2)}) collective-permute-start(f32[512,512]{1,0:T(8,128)} %bitcast.2), channel_id=1, source_target_pairs={{0,4},{4,8},{8,12},{12,16},{16,20},{20,24},{24,28},{1,5},{5,9},{9,... | collective-permute-start | bytes 3145736 | tf_op jit(solution)/shard_map/ppermute | solution.py:14
  11.1 50.2 %collective-permute-start.1 = (f32[512,512]{1,0:T(8,128)}, f32[512,512]{1,0:T(8,128)}, u32[]{:S(2)}, u32[]{:S(2)}) collective-permute-start(f32[512,512]{1,0:T(8,128)} %bitcast.19), channel_id=1, source_target_pairs={{4,0},{8,4},{12,8},{16,12},{20,16},{24,20},{28,24},{5,1},{9,5},{13... | collective-permute-start | bytes 3145736 | tf_op jit(solution)/shard_map/ppermute | solution.py:17
  35.0 19.2 %slice-start = ((s8[10485760]{0:T(1024)(128)(4,1)}), s8[4194304]{0:T(1024)(128)(4,1)S(1)}, s32[]{:S(2)}) async-start(s8[10485760]{0:T(1024)(128)(4,1)} %bitcast.285), calls=%async_computation | async-start | bytes 8388608
  40.0 4.9 %copy-start.3 = (f32[5,256,512]{2,1,0:T(8,128)S(1)}, f32[5,256,512]{2,1,0:T(8,128)}, u32[]{:S(2)}) copy-start(f32[5,256,512]{2,1,0:T(8,128)} %get-tuple-element.22) | copy-start | bytes 7864324
  40.1 14.2 %slice-start.1 = ((s8[10485760]{0:T(1024)(128)(4,1)}), s8[4194304]{0:T(1024)(128)(4,1)S(1)}, s32[]{:S(2)}) async-start(s8[10485760]{0:T(1024)(128)(4,1)} %bitcast.285), calls=%async_computation.1 | async-start | bytes 8388608
  44.9 9.3 %slice-start.2 = ((s8[10485760]{0:T(1024)(128)(4,1)}), s8[2097152]{0:T(1024)(128)(4,1)S(1)}, s32[]{:S(2)}) async-start(s8[10485760]{0:T(1024)(128)(4,1)} %bitcast.285), calls=%async_computation.2 | async-start | bytes 4194304
  65.7 4.7 %copy-start.2 = (f32[2048,512]{1,0:T(8,128)S(1)}, f32[2048,512]{1,0:T(8,128)}, u32[]{:S(2)}) copy-start(f32[2048,512]{1,0:T(8,128)} %param.5) | copy-start | bytes 12582916
  81.7 27.5 %collective-permute-start.2 = (f32[512,512]{1,0:T(8,128)S(1)}, f32[512,512]{1,0:T(8,128)S(1)}, u32[]{:S(2)}, u32[]{:S(2)}) collective-permute-start(f32[512,512]{1,0:T(8,128)S(1)} %get-tuple-element.16), channel_id=1, source_target_pairs={{0,4},{4,8},{8,12},{12,16},{16,20},{20,24},{24,28},{1,5},{5,9},{9,... | collective-permute-start | bytes 3145736 | tf_op jit(solution)/shard_map/ppermute | solution.py:14
  83.6 41.2 %collective-permute-start.3 = (f32[512,512]{1,0:T(8,128)S(1)}, f32[512,512]{1,0:T(8,128)S(1)}, u32[]{:S(2)}, u32[]{:S(2)}) collective-permute-start(f32[512,512]{1,0:T(8,128)S(1)} %get-tuple-element.15), channel_id=1, source_target_pairs={{4,0},{8,4},{12,8},{16,12},{20,16},{24,20},{28,24},{5,1},{9,5},{13... | collective-permute-start | bytes 3145736 | tf_op jit(solution)/shard_map/ppermute | solution.py:17
  130.7 36.4 %slice-start.3 = ((s8[10485760]{0:T(1024)(128)(4,1)}), s8[4194304]{0:T(1024)(128)(4,1)S(1)}, s32[]{:S(2)}) async-start(s8[10485760]{0:T(1024)(128)(4,1)} %bitcast.287), calls=%async_computation.3 | async-start | bytes 8388608
  130.7 36.4 %slice-start.4 = ((s8[10485760]{0:T(1024)(128)(4,1)}), s8[4194304]{0:T(1024)(128)(4,1)S(1)}, s32[]{:S(2)}) async-start(s8[10485760]{0:T(1024)(128)(4,1)} %bitcast.287), calls=%async_computation.4 | async-start | bytes 8388608
  136.0 31.0 %slice-start.5 = ((s8[10485760]{0:T(1024)(128)(4,1)}), s8[2097152]{0:T(1024)(128)(4,1)S(1)}, s32[]{:S(2)}) async-start(s8[10485760]{0:T(1024)(128)(4,1)} %bitcast.287), calls=%async_computation.5 | async-start | bytes 4194304
  139.4 45.5 %copy-start.1 = (f32[2048,512]{1,0:T(8,128)}, f32[2048,512]{1,0:T(8,128)S(1)}, u32[]{:S(2)}) copy-start(f32[2048,512]{1,0:T(8,128)S(1)} %bitcast_add_fusion) | copy-start | bytes 12582916
  139.6 27.5 %collective-permute-start.4 = (f32[512,512]{1,0:T(8,128)S(1)}, f32[512,512]{1,0:T(8,128)S(1)}, u32[]{:S(2)}, u32[]{:S(2)}) collective-permute-start(f32[512,512]{1,0:T(8,128)S(1)} %get-tuple-element.14), channel_id=1, source_target_pairs={{0,4},{4,8},{8,12},{12,16},{16,20},{20,24},{24,28},{1,5},{5,9},{9,... | collective-permute-start | bytes 3145736 | tf_op jit(solution)/shard_map/ppermute | solution.py:14
  141.5 40.9 %collective-permute-start.5 = (f32[512,512]{1,0:T(8,128)S(1)}, f32[512,512]{1,0:T(8,128)S(1)}, u32[]{:S(2)}, u32[]{:S(2)}) collective-permute-start(f32[512,512]{1,0:T(8,128)S(1)} %get-tuple-element.13), channel_id=1, source_target_pairs={{4,0},{8,4},{12,8},{16,12},{20,16},{24,20},{28,24},{5,1},{9,5},{13... | collective-permute-start | bytes 3145736 | tf_op jit(solution)/shard_map/ppermute | solution.py:17
  216.4 4.8 %copy-start.4 = (f32[3,512]{1,0:T(4,128)}, f32[3,512]{1,0:T(4,128)S(1)}, u32[]{:S(2)}) copy-start(f32[3,512]{1,0:T(4,128)S(1)} %fusion.299) | copy-start | bytes 18436
where the time goes:
time: 225 us; the launch traced here: 223 us
  matrix products  92.3 us (41%)
  waiting for transfers between devices  57.8 us (26%)
  blocking collectives  24.7 us (11%)
  starting transfers between devices  19.9 us (9%)
  other arithmetic  18.3 us (8%)
  local copies, waits for them, and re-layouts  6.5 us (3%)
  between operations  3.01 us (1%)
    dot_general x24, matrix products, band_times(): jnp.dot(band_blocks[number], window, precision=lax.Precision.HIGHEST, pre...  76.2 us
    ppermute x3, waiting for transfers between devices, extended(): lax.ppermute(lax.slice_in_dim(block, block.shape[dim] - width, None, axis...  57.8 us
    dot_general x3, matrix products, precondition(): jnp.einsum('jab,jbc->jac', precond_blocks, shaped, precision=lax.Precisio...  16.2 us
    ppermute x3, starting transfers between devices, extended(): lax.ppermute(lax.slice_in_dim(block, 0, width, axis=dim), axis, backward)  14.2 us
    psum x1, blocking collectives, shards(): grand_total = lax.psum(jnp.sum(stacked[ITERS]), 'rhs')  12.6 us
    psum x1, blocking collectives, column_squares(): return lax.psum(partial_value, 'rows')  12.1 us
    reduce_sum x3, other arithmetic, column_squares(): partial_value = jnp.sum(residual * residual, axis=0)  6.86 us
    add x2, other arithmetic, shards(): solution = solution + precondition(precond_blocks, residual)  6.08 us
  transfers between devices with their start and end apart: 6, of which 3 were waited for; matrix products, arithmetic and copies ran while one was open for 27% of the time, Pallas kernels for 0%

commit v1 on v0

v1 whole, which is shorter than its diff:
```python
import jax
import jax.numpy as jnp
from jax import lax
from jax.experimental import pallas as pl
from jax.experimental.pallas import tpu as pltpu
from jax.sharding import PartitionSpec as P

ITERS = 2
REACH = 2
EPS = 1e-06
CHUNKS = 2
LIMIT = 12 * 2**20


def split(value):
    high = value.astype(jnp.bfloat16)
    low = (value - high.astype(jnp.float32)).astype(jnp.bfloat16)
    return high, low


def dot3(left_high, left_low, right_high, right_low):
    def dot(left, right):
        return jnp.dot(left, right, preferred_element_type=jnp.float32)

    return dot(left_high, right_high) + (dot(left_high, right_low) + dot(left_low, right_high))


def whole():
    return pl.BlockSpec(memory_space=pltpu.VMEM)


def scalar():
    return pl.BlockSpec(memory_space=pltpu.SMEM)


def call(kernel, name, out_shapes, in_specs, out_specs, flops, args, grid=(), scratch=(), aliases=None):
    return pl.pallas_call(
        kernel,
        name=name,
        grid=grid,
        in_specs=in_specs,
        out_specs=out_specs,
        out_shape=out_shapes,
        scratch_shapes=scratch,
        input_output_aliases=aliases or {},
        compiler_params=pltpu.CompilerParams(vmem_limit_bytes=LIMIT),
        cost_estimate=pl.CostEstimate(flops=flops, bytes_accessed=0, transcendentals=0),
    )(*args)


def f32(*shape):
    return jax.ShapeDtypeStruct(shape, jnp.float32)


def bf16(*shape):
    return jax.ShapeDtypeStruct(shape, jnp.bfloat16)


def in_hbm(value):
    return pltpu.with_memory_space_constraint(value, pltpu.HBM)


def store_sends(odd_ref, edge_ref, cross_ref, core_ref):
    half = edge_ref.shape[0] // 2
    first = odd_ref[0] * half
    first = pl.multiple_of(first, 256) if half % 256 == 0 else first
    second = half - first
    second = pl.multiple_of(second, 256) if half % 256 == 0 else second
    cross_ref[...] = edge_ref[pl.ds(first, half), :]
    core_ref[...] = edge_ref[pl.ds(second, half), :]


def prepare_kernel(value_ref, high_ref, low_ref):
    high, low = split(value_ref[...])
    high_ref[...] = high
    low_ref[...] = low


def prepare(value):
    count, rows, width = value.shape
    spec = pl.BlockSpec((1, rows, width), lambda i: (i, 0, 0))
    return call(
        prepare_kernel, "prepare", (bf16(*value.shape), bf16(*value.shape)), [spec], (spec, spec),
        value.size, (value,), grid=(count,),
    )


def first_edges(right_side, precond, odd, chunk, width, after):
    nb, br, _ = precond.shape
    edge = REACH * br
    rows = nb * br

    def kernel(odd_ref, right_ref, matrix_ref, *refs):
        edge_ref, cross_ref, core_ref, value, matrix, arrived = refs[-6:]
        columns = pl.ds(chunk * width, width)
        copies = []
        for side, (row, block) in enumerate(((0, 0), (rows - edge, nb - REACH))):
            copies.append(
                (
                    pltpu.make_async_copy(
                        right_ref.at[pl.ds(row, edge), columns], value.at[side], arrived.at[2 * side]
                    ),
                    pltpu.make_async_copy(
                        matrix_ref.at[pl.ds(block, REACH)], matrix.at[side], arrived.at[2 * side + 1]
                    ),
                )
            )
        for pair in copies:
            for copy in pair:
                copy.start()
        for side, pair in enumerate(copies):
            for copy in pair:
                copy.wait()
            for j in range(REACH):
                here = split(matrix[side, j])
                data = split(value[side, j * br : (j + 1) * br, :])
                edge_ref[side * edge + j * br : side * edge + (j + 1) * br, :] = dot3(*here, *data)
        store_sends(odd_ref, edge_ref, cross_ref, core_ref)

    args = [odd, in_hbm(right_side), in_hbm(precond)]
    specs = [scalar()] + [pl.BlockSpec(memory_space=pltpu.HBM)] * 2
    if after is not None:
        args.append(after)
        specs.append(pl.BlockSpec(memory_space=pl.ANY))
    return call(
        kernel, "first_edges",
        (f32(2 * edge, width), f32(edge, width), f32(edge, width)),
        specs,
        (whole(), whole(), whole()),
        6 * 2 * REACH * br * br * width,
        args,
        scratch=[
            pltpu.VMEM((2, edge, width), jnp.float32),
            pltpu.VMEM((2, REACH, br, br), jnp.float32),
            pltpu.SemaphoreType.DMA((4,)),
        ],
    )


def bulk(residual, edge_step, total, band, precond, nb, br, width, chunk, out_width, into, after=None):
    first = total is None
    final = into is not None
    edge = REACH * br
    rows = nb * br
    inner = rows - 2 * edge
    reach = 2 * REACH + 1

    def kernel(*refs):
        refs = list(refs)
        if first:
            right_ref = refs.pop(0)
            edge_of = lambda j: right_ref.at[pl.ds(j * br, br), :]
            inner_of = edge_of
        else:
            redge_ref, rinner_ref = refs.pop(0), refs.pop(0)
        dedge_ref = refs.pop(0)
        if not first:
            total_ref = refs.pop(0)
        ah_ref, al_ref, mh_ref, ml_ref = [refs.pop(0) for _ in range(4)]
        if final and into is not True:
            refs.pop(0)
        if after is not None:
            refs.pop(0)
        outedge_ref, outinner_ref, outtotal_ref = [refs.pop(0) for _ in range(3)]
        if not first:
            squares_ref = refs.pop(0)
        dh_ref, dl_ref = refs

        def rows_of(j):
            if first:
                return right_ref[pl.ds(pl.multiple_of(j * br, br), br), :]
            return rinner_ref[pl.ds(pl.multiple_of((j - REACH) * br, br), br), :]

        def edge_rows(j):
            if first:
                return right_ref[j * br : (j + 1) * br, :]
            k = j if j < REACH else j - nb + 2 * REACH
            return redge_ref[k * br : (k + 1) * br, :]

        for j in list(range(REACH)) + list(range(nb - REACH, nb)):
            k = j if j < REACH else j - nb + 2 * REACH
            d = dedge_ref[k * br : (k + 1) * br, :]
            high, low = split(d)
            dh_ref[j * br : (j + 1) * br, :] = high
            dl_ref[j * br : (j + 1) * br, :] = low
            if first:
                outtotal_ref[j * br : (j + 1) * br, :] = d
            else:
                outtotal_ref[j * br : (j + 1) * br, :] = total_ref[j * br : (j + 1) * br, :] + d

        def make(j):
            value = rows_of(j)
            d = dot3(mh_ref[j], ml_ref[j], *split(value))
            high, low = split(d)
            here = pl.ds(pl.multiple_of(j * br, br), br)
            dh_ref[here, :] = high
            dl_ref[here, :] = low
            if first:
                outtotal_ref[here, :] = d
            else:
                outtotal_ref[here, :] = total_ref[here, :] + d

        for j in range(REACH, nb - REACH):
            make(j)

        if not first:
            squares = jnp.zeros((8, width), jnp.float32)
            for j in range(nb):
                value = edge_rows(j) if j < REACH or j >= nb - REACH else rows_of(j)
                squares = squares + jnp.sum((value * value).reshape(-1, 8, width), axis=0)
            squares_ref[...] = jnp.sum(squares, axis=0, keepdims=True)

        for j in range(nb):
            start, stop = max(0, REACH - j), min(reach, nb + REACH - j)
            here = pl.ds((j + start - REACH) * br, (stop - start) * br)
            columns = slice(start * br, stop * br)
            product = dot3(ah_ref[j, :, columns], al_ref[j, :, columns], dh_ref[here, :], dl_ref[here, :])
            if j < REACH or j >= nb - REACH:
                k = j if j < REACH else j - nb + 2 * REACH
                outedge_ref[k * br : (k + 1) * br, :] = edge_rows(j) - product
            else:
                outinner_ref[(j - REACH) * br : (j - REACH + 1) * br, :] = rows_of(j) - product

    one = (1,)
    full = lambda shape: pl.BlockSpec(shape, lambda i: (0,) * len(shape))
    if first:
        specs = [pl.BlockSpec((rows, width), lambda i: (0, chunk))]
    else:
        specs = [whole(), whole()]
    specs += [whole()]
    if not first:
        specs += [whole()]
    args = [*residual, edge_step] + ([] if first else [total]) + [*band, *precond]
    specs += [whole()] * 4
    aliases = {}
    total_shape = f32(rows, width)
    total_spec = whole()
    if final:
        total_shape = f32(rows, out_width)
        total_spec = pl.BlockSpec((rows, width), lambda i: (0, chunk))
        if into is not True:
            aliases = {len(args): 2}
            args.append(into)
            specs.append(pl.BlockSpec(memory_space=pl.ANY))
    if after is not None:
        args.append(after)
        specs.append(pl.BlockSpec(memory_space=pl.ANY))
    shapes = [f32(2 * edge, width), f32(inner, width), total_shape]
    outs = [whole(), whole(), total_spec]
    if not first:
        shapes.append(f32(1, width))
        outs.append(whole())
    products = (nb - 2 * REACH) + nb * reach - REACH * (REACH + 1)
    return call(
        kernel, "bulk", tuple(shapes), specs, tuple(outs), 6 * products * br * br * width, args, grid=one,
        scratch=[pltpu.VMEM((rows, width), jnp.bfloat16), pltpu.VMEM((rows, width), jnp.bfloat16)],
        aliases=aliases,
    )


def edges(partial_edge, cross, core, band, precond, odd, nb, br, width, after, last=None):
    edge = REACH * br

    def kernel(*refs):
        refs = list(refs)
        odd_ref, part_ref, cross_ref, core_ref, ah_ref, al_ref = [refs.pop(0) for _ in range(6)]
        if last is None:
            mh_ref, ml_ref = refs.pop(0), refs.pop(0)
        else:
            inner_ref = refs.pop(0)
            known = [refs.pop(0) for _ in last[1]]
        refs.pop(0)
        if last is None:
            out_ref, step_ref, sendx_ref, sends_ref, hh_ref, hl_ref = refs
        else:
            out_ref, message_ref, hh_ref, hl_ref = refs
        odd_value = odd_ref[0]
        for ref, slot in ((cross_ref, odd_value), (core_ref, 1 - odd_value)):
            high, low = split(ref[...])
            hh_ref[pl.ds(pl.multiple_of(slot * edge, 8), edge), :] = high
            hl_ref[pl.ds(pl.multiple_of(slot * edge, 8), edge), :] = low
        squares = jnp.zeros((8, width), jnp.float32)
        for k in range(2 * REACH):
            j = k if k < REACH else k + nb - 2 * REACH
            if k < REACH:
                columns = slice(0, (REACH - k) * br)
                here = slice(k * br, edge)
            else:
                reached = k - REACH + 1
                columns = slice((2 * REACH + 1 - reached) * br, (2 * REACH + 1) * br)
                here = slice(edge, edge + reached * br)
            product = dot3(ah_ref[j, :, columns], al_ref[j, :, columns], hh_ref[here, :], hl_ref[here, :])
            value = part_ref[k * br : (k + 1) * br, :] - product
            out_ref[k * br : (k + 1) * br, :] = value
            if last is not None:
                squares = squares + jnp.sum((value * value).reshape(-1, 8, width), axis=0)
            else:
                step_ref[k * br : (k + 1) * br, :] = dot3(mh_ref[j], ml_ref[j], *split(value))
        if last is not None:
            for j in range(nb - 2 * REACH):
                value = inner_ref[j * br : (j + 1) * br, :]
                squares = squares + jnp.sum((value * value).reshape(-1, 8, width), axis=0)
            own = jnp.sum(squares, axis=0, keepdims=True)
            if not known:
                message_ref[...] = own
            for k, piece in enumerate([ref[...] for ref in known] + [own] if known else []):
                shape = (message_ref.shape[0], 1, width)
                message_ref[:, :, k * width : (k + 1) * width] = jnp.broadcast_to(piece[None], shape)
        else:
            store_sends(odd_ref, step_ref, sendx_ref, sends_ref)

    products = REACH * (REACH + 1) + (2 * REACH if last is None else 0)
    args = [odd, partial_edge, cross, core, *band]
    if last is not None:
        devices, known_sums, inner_rows = last[0], last[1], last[2]
        args += [inner_rows, *known_sums]
        sent = f32(devices, 1, (1 + len(known_sums)) * width) if known_sums else f32(1, width)
        shapes = (f32(2 * edge, width), sent)
    else:
        args += [*precond]
        shapes = (f32(2 * edge, width), f32(2 * edge, width), f32(edge, width), f32(edge, width))
    specs = [scalar()] + [whole()] * (len(args) - 1) + [pl.BlockSpec(memory_space=pl.ANY)]
    args.append(after)
    return call(
        kernel, "edges" if last is None else "edges_last", shapes, specs,
        tuple(whole() for _ in shapes), 6 * products * br * br * width, args,
        scratch=[pltpu.VMEM((2 * edge, width), jnp.bfloat16), pltpu.VMEM((2 * edge, width), jnp.bfloat16)],
    )


def scale_out(state, gathered, place, count, across, nb, br, width):
    rows = nb * br
    edge = REACH * br
    inner_steps = (nb - 2 * REACH) // REACH
    steps = inner_steps + 2
    part = width // CHUNKS
    total_rows = count * rows

    def kernel(place_ref, *refs):
        pieces = refs[: 2 * CHUNKS]
        here_ref, out_ref, history_ref, overall_ref, inverse_ref = refs[2 * CHUNKS :]
        step = pl.program_id(0)

        @pl.when(step == 0)
        def _():
            place_value = place_ref[0]
            for sweep in range(ITERS + 1):
                columns = slice(sweep * width, (sweep + 1) * width)
                value = here_ref[place_value, :, columns]
                for row in range(1, count):
                    value = value + here_ref[place_value + row * across, :, columns]
                root = jnp.sqrt(value / total_rows + EPS)
                history_ref[sweep : sweep + 1, :] = root
            inverse_ref[...] = 1.0 / root
            everything = jnp.sum(here_ref[:, :, ITERS * width :], axis=0)
            total = jnp.sum(everything, axis=1, keepdims=True)
            overall_ref[...] = jnp.sqrt(total / (total_rows * across * width) + EPS)

        def write(inner):
            for c in range(CHUNKS):
                columns = slice(c * part, (c + 1) * part)
                ref = pieces[2 * c + (1 if inner else 0)]
                out_ref[:, columns] = ref[...] * inverse_ref[:, columns]

        inside = (step > 0) & (step < steps - 1)
        pl.when(inside)(lambda: write(True))
        pl.when(jnp.logical_not(inside))(lambda: write(False))

    args, specs = [place], [scalar()]
    for outer, inner in state:
        args += [outer, inner]
        specs += [
            pl.BlockSpec((edge, part), lambda i: (i // (steps - 1), 0)),
            pl.BlockSpec((edge, part), lambda i: (jnp.clip(i - 1, 0, inner_steps - 1), 0)),
        ]
    return call(
        kernel, "scale_out", (f32(rows, width), f32(ITERS + 1, width), f32(1, 1)), specs + [whole()],
        (pl.BlockSpec((edge, width), lambda i: (i, 0)), whole(), whole()),
        rows * width, args + [gathered], grid=(steps,),
        scratch=[pltpu.VMEM((1, width), jnp.float32)],
    )


def swaps(count):
    core = [(i, i ^ 1) for i in range(count) if (i ^ 1) < count]
    cross = []
    for i in range(1, count - 1, 2):
        cross += [(i, i + 1), (i + 1, i)]
    return core, cross


def shards(band_blocks, precond_blocks, right_side):
    nb, br, _ = precond_blocks.shape
    width = right_side.shape[1]
    part = width // CHUNKS
    count = lax.axis_size("rows")
    across = lax.axis_size("rhs")
    core_pairs, cross_pairs = swaps(count)
    odd = (lax.axis_index("rows") % 2).astype(jnp.int32)[None]

    def exchange(cross_send, core_send):
        return lax.ppermute(cross_send, "rows", cross_pairs), lax.ppermute(core_send, "rows", core_pairs)

    place = lax.axis_index("rhs").astype(jnp.int32)[None]
    step, halo = [], []
    for c in range(CHUNKS):
        edge_step, cross_send, core_send = first_edges(
            right_side, precond_blocks, odd, c, part, step[-1] if c else None
        )
        step.append(edge_step)
        halo.append(exchange(cross_send, core_send))
    band = prepare(band_blocks)
    precond = prepare(precond_blocks)
    state = [None] * CHUNKS
    sums = [[None] * CHUNKS for _ in range(ITERS)]
    total = [None] * CHUNKS
    answer, after = None, step[-1]
    for c in range(CHUNKS):
        outer, inner, total[c] = bulk(
            (right_side,), step[c], None, band, precond, nb, br, part, c, width, None, after
        )
        state[c] = (outer, inner)
        after = outer
    for sweep in range(ITERS):
        for c in range(CHUNKS):
            outer, inner = state[c]
            outer, step[c], cross_send, core_send = edges(
                outer, *halo[c], band, precond, odd, nb, br, part, after
            )
            halo[c] = exchange(cross_send, core_send)
            into = None
            if sweep == ITERS - 1:
                into = True if answer is None else answer
            outer, inner, total[c], sums[sweep][c] = bulk(
                (outer, inner), step[c], total[c], band, precond, nb, br, part, c, width, into
            )
            if into is not None:
                answer = total[c]
            after = outer
            state[c] = (outer, inner)
    known = [s for row in sums for s in row]
    for c in range(CHUNKS):
        outer, inner = state[c]
        send = known if c == CHUNKS - 1 else []
        outer, message = edges(
            outer, *halo[c], band, precond, odd, nb, br, part, after, (count * across, send, inner)
        )
        known.append(message)
        after = outer
        state[c] = (outer, inner)
    gathered = lax.all_to_all(message, ("rows", "rhs"), 0, 0, tiled=True)
    scaled, history, overall = scale_out(state, gathered, place, count, across, nb, br, width)
    return (answer, scaled, history, overall.reshape(()))


def solution(mesh):
    in_specs = (P("rows", None, None), P("rows", None, None), P("rows", "rhs"))
    out_specs = (P("rows", "rhs"), P("rows", "rhs"), P(None, "rhs"), P())
    return jax.shard_map(shards, mesh=mesh, in_specs=in_specs, out_specs=out_specs, check_vma=False)
```

time: 225 us -> 98.9 us (0.44)
  the two profiles are of different devices: /device:TPU:4 before, /device:TPU:0 now
where the time goes in v1:
time: 98.9 us; the launch traced here: 98.5 us
  Pallas kernels  47.6 us (48%)
  starting transfers between devices  37.8 us (38%)
  waiting for transfers between devices  9.33 us (9%)
  local copies, waits for them, and re-layouts  2.85 us (3%)
    pallas_call x17, Pallas kernels, call(): pl.pallas_call(kernel, name=name, grid=grid, in_specs=in_specs, out_specs...  47.6 us
    ppermute x6, starting transfers between devices, exchange(): lax.ppermute(core_send, 'rows', core_pairs)  17.9 us
    all_to_all x1, starting transfers between devices, shards(): gathered = lax.all_to_all(message, ('rows', 'rhs'), 0, 0, tiled=True)  15.2 us
    all_to_all x1, waiting for transfers between devices, shards(): gathered = lax.all_to_all(message, ('rows', 'rhs'), 0, 0, tiled=True)  9.3 us
    ppermute x6, starting transfers between devices, exchange(): lax.ppermute(cross_send, 'rows', cross_pairs)  4.7 us
    unnamed x10, local copies, waits for them, and re-layouts  2.85 us
  transfers between devices with their start and end apart: 13, of which 1 were waited for; matrix products, arithmetic and copies ran while one was open for 0% of the time, Pallas kernels for 42%

profile of v1, /device:TPU:0, one launch (start us, length us, event | category | flops | bytes accessed | tf_op | source)
XLA Modules:
  0.0 98.5 jit_solution(8307787915907232840)
XLA Ops:
  0.7 2.3 %first_edges.2 = (f32[1024,256]{1,0:T(8,128)S(1)}, f32[512,256]{1,0:T(8,128)S(1)}, f32[512,256]{1,0:T(8,128)S(1)}) custom-call(s32[1]{0:T(128)} %bitcast.odd_ref.refs_0_, f32[2048,512]{1,0:T(8,128)} %refs_0_.3, f32[8,256,256]{2,1,0:T(8,128)} %value_ref.3), custom_call_target="tpu_custom_call" | custom-call | flops 402653184 | tf_op jit(solution)/shard_map/first_edges/pallas_call | solution.py:37
  3.8 4.5 %collective-permute-start.3 = (f32[512,256]{1,0:T(8,128)S(1)}, f32[512,256]{1,0:T(8,128)S(1)}, u32[]{:S(2)}, u32[]{:S(2)}) collective-permute-start(f32[512,256]{1,0:T(8,128)S(1)} %get-tuple-element.70), channel_id=1, source_target_pairs={{0,4},{4,0},{8,12},{12,8},{16,20},{20,16},{24,28},{28,24},{1,5},{5... | collective-permute-start | bytes 1572872 | tf_op jit(solution)/shard_map/ppermute | solution.py:402
  8.2 2.1 %first_edges.3 = (f32[1024,256]{1,0:T(8,128)S(1)}, f32[512,256]{1,0:T(8,128)S(1)}, f32[512,256]{1,0:T(8,128)S(1)}) custom-call(s32[1]{0:T(128)} %bitcast.odd_ref.refs_0_, f32[2048,512]{1,0:T(8,128)} %refs_0_.3, f32[8,256,256]{2,1,0:T(8,128)} %value_ref.3, f32[1024,256]{1,0:T(8,128)S(1)} %get-tuple-element.59.refs_0_.refs_1_), custom_call_target="tpu_custom_call" | custom-call | flops 402653184 | tf_op jit(solution)/shard_map/first_edges/pallas_call | solution.py:37
  11.1 2.9 %collective-permute-start.1 = (f32[512,256]{1,0:T(8,128)S(1)}, f32[512,256]{1,0:T(8,128)S(1)}, u32[]{:S(2)}, u32[]{:S(2)}) collective-permute-start(f32[512,256]{1,0:T(8,128)S(1)} %get-tuple-element.68), channel_id=1, source_target_pairs={{0,4},{4,0},{8,12},{12,8},{16,20},{20,16},{24,28},{28,24},{1,5},{5... | collective-permute-start | bytes 1572872 | tf_op jit(solution)/shard_map/ppermute | solution.py:402
  14.4 1.5 %prepare.2 = (bf16[8,256,1280]{2,1,0:T(8,128)(2,1)S(1)}, bf16[8,256,1280]{2,1,0:T(8,128)(2,1)S(1)}) custom-call(f32[8,256,1280]{2,1,0:T(8,128)S(1)} %copy-done.2), custom_call_target="tpu_custom_call" | custom-call | flops 2621440 | tf_op jit(solution)/shard_map/prepare/pallas_call | solution.py:37
  16.6 4.1 %bulk.6 = (f32[1024,256]{1,0:T(8,128)S(1)}, f32[1024,256]{1,0:T(8,128)S(1)}, f32[2048,256]{1,0:T(8,128)S(1)}) custom-call(f32[2048,512]{1,0:T(8,128)S(1)} %copy-done, f32[1024,256]{1,0:T(8,128)S(1)} %get-tuple-element.59.refs_0_.refs_1_, bf16[8,256,1280]{2,1,0:T(8,128)(2,1)S(1)} %get-tuple-element.61.refs_2_.refs_4_, ...), custom_call_target="tpu_custom_call" | custom-call | flops 3825205248 | tf_op jit(solution)/shard_map/bulk/pallas_call | solution.py:37
  20.7 4.1 %bulk.7 = (f32[1024,256]{1,0:T(8,128)S(1)}, f32[1024,256]{1,0:T(8,128)S(1)}, f32[2048,256]{1,0:T(8,128)S(1)}) custom-call(f32[2048,512]{1,0:T(8,128)S(1)} %copy-done, f32[1024,256]{1,0:T(8,128)S(1)} %get-tuple-element.60.refs_6_.refs_1_, bf16[8,256,1280]{2,1,0:T(8,128)(2,1)S(1)} %get-tuple-element.61.refs_2_.refs_4_, ...), custom_call_target="tpu_custom_call" | custom-call | flops 3825205248 | tf_op jit(solution)/shard_map/bulk/pallas_call | solution.py:37
  24.8 2.3 %edges.4 = (f32[1024,256]{1,0:T(8,128)S(1)}, f32[1024,256]{1,0:T(8,128)S(1)}, f32[512,256]{1,0:T(8,128)S(1)}, f32[512,256]{1,0:T(8,128)S(1)}) custom-call(s32[1]{0:T(128)} %bitcast.odd_ref.refs_0_, f32[1024,256]{1,0:T(8,128)S(1)} %get-tuple-element.65.refs_6_.refs_1_, f32[512,256]{1,0:T(8,128)S(1)} %collective-permute-done.2.refs_2_, ...), custom_call_target="tpu_custom_call" | custom-call | flops 1006632960 | tf_op jit(solution)/shard_map/edges/pallas_call | solution.py:37
  28.0 2.9 %collective-permute-start.7 = (f32[512,256]{1,0:T(8,128)S(1)}, f32[512,256]{1,0:T(8,128)S(1)}, u32[]{:S(2)}, u32[]{:S(2)}) collective-permute-start(f32[512,256]{1,0:T(8,128)S(1)} %get-tuple-element.84), channel_id=1, source_target_pairs={{0,4},{4,0},{8,12},{12,8},{16,20},{20,16},{24,28},{28,24},{1,5},{5... | collective-permute-start | bytes 1572872 | tf_op jit(solution)/shard_map/ppermute | solution.py:402
  30.8 4.2 %bulk.8 = (f32[1024,256]{1,0:T(8,128)S(1)}, f32[1024,256]{1,0:T(8,128)S(1)}, f32[2048,256]{1,0:T(8,128)S(1)}, f32[1,256]{1,0:T(1,128)S(1)}) custom-call(f32[1024,256]{1,0:T(8,128)S(1)} %get-tuple-element.71.refs_0_, f32[1024,256]{1,0:T(8,128)S(1)} %get-tuple-element.72.refs_1_, f32[1024,256]{1,0:T(8,128)S(1)} %get-tuple-element.73.refs_2_, ...), custom_call_target="tpu_custom_call" | custom-call | flops 3825205248 | tf_op jit(solution)/shard_map/bulk/pallas_call | solution.py:37
  35.1 2.3 %edges.5 = (f32[1024,256]{1,0:T(8,128)S(1)}, f32[1024,256]{1,0:T(8,128)S(1)}, f32[512,256]{1,0:T(8,128)S(1)}, f32[512,256]{1,0:T(8,128)S(1)}) custom-call(s32[1]{0:T(128)} %bitcast.odd_ref.refs_0_, f32[1024,256]{1,0:T(8,128)S(1)} %get-tuple-element.66.refs_8_.refs_1_, f32[512,256]{1,0:T(8,128)S(1)} %collective-permute-done.refs_2_, ...), custom_call_target="tpu_custom_call" | custom-call | flops 1006632960 | tf_op jit(solution)/shard_map/edges/pallas_call | solution.py:37
  38.1 2.4 %collective-permute-start.5 = (f32[512,256]{1,0:T(8,128)S(1)}, f32[512,256]{1,0:T(8,128)S(1)}, u32[]{:S(2)}, u32[]{:S(2)}) collective-permute-start(f32[512,256]{1,0:T(8,128)S(1)} %get-tuple-element.82), channel_id=1, source_target_pairs={{0,4},{4,0},{8,12},{12,8},{16,20},{20,16},{24,28},{28,24},{1,5},{5... | collective-permute-start | bytes 1572872 | tf_op jit(solution)/shard_map/ppermute | solution.py:402
  40.4 4.1 %bulk.9 = (f32[1024,256]{1,0:T(8,128)S(1)}, f32[1024,256]{1,0:T(8,128)S(1)}, f32[2048,256]{1,0:T(8,128)S(1)}, f32[1,256]{1,0:T(1,128)S(1)}) custom-call(f32[1024,256]{1,0:T(8,128)S(1)} %get-tuple-element.76.refs_0_, f32[1024,256]{1,0:T(8,128)S(1)} %get-tuple-element.77.refs_1_, f32[1024,256]{1,0:T(8,128)S(1)} %get-tuple-element.78.refs_2_, ...), custom_call_target="tpu_custom_call" | custom-call | flops 3825205248 | tf_op jit(solution)/shard_map/bulk/pallas_call | solution.py:37
  44.6 2.3 %edges.6 = (f32[1024,256]{1,0:T(8,128)S(1)}, f32[1024,256]{1,0:T(8,128)S(1)}, f32[512,256]{1,0:T(8,128)S(1)}, f32[512,256]{1,0:T(8,128)S(1)}) custom-call(s32[1]{0:T(128)} %bitcast.odd_ref.refs_0_, f32[1024,256]{1,0:T(8,128)S(1)} %get-tuple-element.75.refs_8_.refs_1_, f32[512,256]{1,0:T(8,128)S(1)} %collective-permute-done.6.refs_2_, ...), custom_call_target="tpu_custom_call" | custom-call | flops 1006632960 | tf_op jit(solution)/shard_map/edges/pallas_call | solution.py:37
  47.8 2.9 %collective-permute-start.9 = (f32[512,256]{1,0:T(8,128)S(1)}, f32[512,256]{1,0:T(8,128)S(1)}, u32[]{:S(2)}, u32[]{:S(2)}) collective-permute-start(f32[512,256]{1,0:T(8,128)S(1)} %get-tuple-element.97), channel_id=1, source_target_pairs={{0,4},{4,0},{8,12},{12,8},{16,20},{20,16},{24,28},{28,24},{1,5},{5... | collective-permute-start | bytes 1572872 | tf_op jit(solution)/shard_map/ppermute | solution.py:402
  50.7 5.1 %bulk.10 = (f32[1024,256]{1,0:T(8,128)S(1)}, f32[1024,256]{1,0:T(8,128)S(1)}, f32[2048,512]{1,0:T(8,128)}, f32[1,256]{1,0:T(1,128)S(1)}) custom-call(f32[1024,256]{1,0:T(8,128)S(1)} %get-tuple-element.85.refs_0_, f32[1024,256]{1,0:T(8,128)S(1)} %get-tuple-element.86.refs_1_, f32[1024,256]{1,0:T(8,128)S(1)} %get-tuple-element.87.refs_2_, ...), custom_call_target="tpu_custom_call" | custom-call | flops 3825205248 | tf_op jit(solution)/shard_map/bulk/pallas_call | solution.py:37
  55.9 2.3 %edges.7 = (f32[1024,256]{1,0:T(8,128)S(1)}, f32[1024,256]{1,0:T(8,128)S(1)}, f32[512,256]{1,0:T(8,128)S(1)}, f32[512,256]{1,0:T(8,128)S(1)}) custom-call(s32[1]{0:T(128)} %bitcast.odd_ref.refs_0_, f32[1024,256]{1,0:T(8,128)S(1)} %get-tuple-element.80.refs_8_.refs_1_, f32[512,256]{1,0:T(8,128)S(1)} %collective-permute-done.4.refs_2_, ...), custom_call_target="tpu_custom_call" | custom-call | flops 1006632960 | tf_op jit(solution)/shard_map/edges/pallas_call | solution.py:37
  58.8 2.4 %collective-permute-start.11 = (f32[512,256]{1,0:T(8,128)S(1)}, f32[512,256]{1,0:T(8,128)S(1)}, u32[]{:S(2)}, u32[]{:S(2)}) collective-permute-start(f32[512,256]{1,0:T(8,128)S(1)} %get-tuple-element.102), channel_id=1, source_target_pairs={{0,4},{4,0},{8,12},{12,8},{16,20},{20,16},{24,28},{28,24},{1,5},{5... | collective-permute-start | bytes 1572872 | tf_op jit(solution)/shard_map/ppermute | solution.py:402
  61.2 5.1 %bulk.11 = (f32[1024,256]{1,0:T(8,128)S(1)}, f32[1024,256]{1,0:T(8,128)S(1)}, f32[2048,512]{1,0:T(8,128)}, f32[1,256]{1,0:T(1,128)S(1)}) custom-call(f32[1024,256]{1,0:T(8,128)S(1)} %get-tuple-element.90.refs_0_, f32[1024,256]{1,0:T(8,128)S(1)} %get-tuple-element.91.refs_1_, ...), custom_call_target="tpu_custom_call", output_to_operand_aliasing={{2}: (8, {})} | custom-call | flops 3825205248 | tf_op jit(solution)/shard_map/bulk/pallas_call | solution.py:37
  67.4 1.8 %edges_last.3 = (f32[1024,256]{1,0:T(8,128)S(1)}, f32[32,1,1536]{2,1,0:T(1,128)}) custom-call(s32[1]{0:T(128)} %bitcast.odd_ref.refs_0_, f32[1024,256]{1,0:T(8,128)S(1)} %get-tuple-element.99.refs_7_.refs_1_, f32[512,256]{1,0:T(8,128)S(1)} %collective-permute-done.10.refs_2_, f32[512,256]{1,0:T(8,128)S(1)} %collective-permute-done.11.refs_3_, ...), custom_call_target="tpu_custom_call" | custom-call | flops 603979776 | tf_op jit(solution)/shard_map/edges_last/pallas_call | solution.py:37
  70.1 15.2 %all-to-all-start = ((f32[32,1,1536]{2,1,0:T(1,128)}), f32[32,1,1536]{2,1,0:T(1,128)S(1)}, u32[]{:S(2)}, u32[]{:S(2)}) async-start(f32[32,1,1536]{2,1,0:T(1,128)} %get-tuple-element.110), calls=%async_computation | async-start | bytes 393216 | tf_op jit(solution)/shard_map/all_to_all | solution.py:451
  85.4 9.3 %all-to-all-done.refs_4_ = f32[32,1,1536]{2,1,0:T(1,128)S(1)} async-done(((f32[32,1,1536]{2,1,0:T(1,128)}), f32[32,1,1536]{2,1,0:T(1,128)S(1)}, u32[]{:S(2)}, u32[]{:S(2)}) %all-to-all-start) | async-done | bytes 196640 | tf_op jit(solution)/shard_map/all_to_all | solution.py:451
  94.7 1.2 %copy-done.4 = f32[1024,256]{1,0:T(8,128)S(1)} copy-done((f32[1024,256]{1,0:T(8,128)S(1)}, f32[1024,256]{1,0:T(8,128)}, u32[]{:S(2)}) %copy-start.4) | copy-done | bytes 1048600
  95.9 2.6 %scale_out.1 = (f32[2048,512]{1,0:T(8,128)}, f32[3,512]{1,0:T(4,128)}, f32[1,1]{1,0:T(1,128)}) custom-call(s32[1]{0:T(128)} %bitcast.1.place_ref, f32[1024,256]{1,0:T(8,128)S(1)} %get-tuple-element.100.refs_12_.refs_0_, f32[1024,256]{1,0:T(8,128)S(1)} %get-tuple-element.98.refs_6_.refs_1_, f32[1024,256]{1,0:T(8,128)S(1)} %copy-done.4, ...), custom_call_target="tpu_custom_call" | custom-call | flops 1048576 | tf_op jit(solution)/shard_map/scale_out/pallas_call | solution.py:37
  (29 shorter events, 7.8 us)
Async XLA Ops:
  0.6 13.7 %copy-start.2 = (f32[8,256,1280]{2,1,0:T(8,128)S(1)}, f32[8,256,1280]{2,1,0:T(8,128)}, u32[]{:S(2)}) copy-start(f32[8,256,1280]{2,1,0:T(8,128)} %value_ref.2) | copy-start | bytes 31457284
  2.9 11.0 %copy-start.1 = (f32[8,256,256]{2,1,0:T(8,128)S(1)}, f32[8,256,256]{2,1,0:T(8,128)}, u32[]{:S(2)}) copy-start(f32[8,256,256]{2,1,0:T(8,128)} %value_ref.3) | copy-start | bytes 6291460
  2.9 21.9 %collective-permute-start.2 = (f32[512,256]{1,0:T(8,128)S(1)}, f32[512,256]{1,0:T(8,128)S(1)}, u32[]{:S(2)}, u32[]{:S(2)}) collective-permute-start(f32[512,256]{1,0:T(8,128)S(1)} %get-tuple-element.69), channel_id=1, source_target_pairs={{4,8},{8,4},{12,16},{16,12},{20,24},{24,20},{5,9},{9,5},{13,17},{1... | collective-permute-start | bytes 1572872 | tf_op jit(solution)/shard_map/ppermute | solution.py:402
  3.8 21.0 %collective-permute-start.3 = (f32[512,256]{1,0:T(8,128)S(1)}, f32[512,256]{1,0:T(8,128)S(1)}, u32[]{:S(2)}, u32[]{:S(2)}) collective-permute-start(f32[512,256]{1,0:T(8,128)S(1)} %get-tuple-element.70), channel_id=1, source_target_pairs={{0,4},{4,0},{8,12},{12,8},{16,20},{20,16},{24,28},{28,24},{1,5},{5... | collective-permute-start | bytes 1572872 | tf_op jit(solution)/shard_map/ppermute | solution.py:402
  10.4 24.7 %collective-permute-start = (f32[512,256]{1,0:T(8,128)S(1)}, f32[512,256]{1,0:T(8,128)S(1)}, u32[]{:S(2)}, u32[]{:S(2)}) collective-permute-start(f32[512,256]{1,0:T(8,128)S(1)} %get-tuple-element.67), channel_id=1, source_target_pairs={{4,8},{8,4},{12,16},{16,12},{20,24},{24,20},{5,9},{9,5},{13,17},{1... | collective-permute-start | bytes 1572872 | tf_op jit(solution)/shard_map/ppermute | solution.py:402
  11.1 24.0 %collective-permute-start.1 = (f32[512,256]{1,0:T(8,128)S(1)}, f32[512,256]{1,0:T(8,128)S(1)}, u32[]{:S(2)}, u32[]{:S(2)}) collective-permute-start(f32[512,256]{1,0:T(8,128)S(1)} %get-tuple-element.68), channel_id=1, source_target_pairs={{0,4},{4,0},{8,12},{12,8},{16,20},{20,16},{24,28},{28,24},{1,5},{5... | collective-permute-start | bytes 1572872 | tf_op jit(solution)/shard_map/ppermute | solution.py:402
  14.4 2.2 %copy-start = (f32[2048,512]{1,0:T(8,128)S(1)}, f32[2048,512]{1,0:T(8,128)}, u32[]{:S(2)}) copy-start(f32[2048,512]{1,0:T(8,128)} %refs_0_.3) | copy-start | bytes 12582916
  27.1 17.5 %collective-permute-start.6 = (f32[512,256]{1,0:T(8,128)S(1)}, f32[512,256]{1,0:T(8,128)S(1)}, u32[]{:S(2)}, u32[]{:S(2)}) collective-permute-start(f32[512,256]{1,0:T(8,128)S(1)} %get-tuple-element.83), channel_id=1, source_target_pairs={{4,8},{8,4},{12,16},{16,12},{20,24},{24,20},{5,9},{9,5},{13,17},{1... | collective-permute-start | bytes 1572872 | tf_op jit(solution)/shard_map/ppermute | solution.py:402
  28.0 16.6 %collective-permute-start.7 = (f32[512,256]{1,0:T(8,128)S(1)}, f32[512,256]{1,0:T(8,128)S(1)}, u32[]{:S(2)}, u32[]{:S(2)}) collective-permute-start(f32[512,256]{1,0:T(8,128)S(1)} %get-tuple-element.84), channel_id=1, source_target_pairs={{0,4},{4,0},{8,12},{12,8},{16,20},{20,16},{24,28},{28,24},{1,5},{5... | collective-permute-start | bytes 1572872 | tf_op jit(solution)/shard_map/ppermute | solution.py:402
  37.4 18.5 %collective-permute-start.4 = (f32[512,256]{1,0:T(8,128)S(1)}, f32[512,256]{1,0:T(8,128)S(1)}, u32[]{:S(2)}, u32[]{:S(2)}) collective-permute-start(f32[512,256]{1,0:T(8,128)S(1)} %get-tuple-element.81), channel_id=1, source_target_pairs={{4,8},{8,4},{12,16},{16,12},{20,24},{24,20},{5,9},{9,5},{13,17},{1... | collective-permute-start | bytes 1572872 | tf_op jit(solution)/shard_map/ppermute | solution.py:402
  38.1 17.8 %collective-permute-start.5 = (f32[512,256]{1,0:T(8,128)S(1)}, f32[512,256]{1,0:T(8,128)S(1)}, u32[]{:S(2)}, u32[]{:S(2)}) collective-permute-start(f32[512,256]{1,0:T(8,128)S(1)} %get-tuple-element.82), channel_id=1, source_target_pairs={{0,4},{4,0},{8,12},{12,8},{16,20},{20,16},{24,28},{28,24},{1,5},{5... | collective-permute-start | bytes 1572872 | tf_op jit(solution)/shard_map/ppermute | solution.py:402
  46.9 19.4 %collective-permute-start.8 = (f32[512,256]{1,0:T(8,128)S(1)}, f32[512,256]{1,0:T(8,128)S(1)}, u32[]{:S(2)}, u32[]{:S(2)}) collective-permute-start(f32[512,256]{1,0:T(8,128)S(1)} %get-tuple-element.96), channel_id=1, source_target_pairs={{4,8},{8,4},{12,16},{16,12},{20,24},{24,20},{5,9},{9,5},{13,17},{1... | collective-permute-start | bytes 1572872 | tf_op jit(solution)/shard_map/ppermute | solution.py:402
  47.8 18.5 %collective-permute-start.9 = (f32[512,256]{1,0:T(8,128)S(1)}, f32[512,256]{1,0:T(8,128)S(1)}, u32[]{:S(2)}, u32[]{:S(2)}) collective-permute-start(f32[512,256]{1,0:T(8,128)S(1)} %get-tuple-element.97), channel_id=1, source_target_pairs={{0,4},{4,0},{8,12},{12,8},{16,20},{20,16},{24,28},{28,24},{1,5},{5... | collective-permute-start | bytes 1572872 | tf_op jit(solution)/shard_map/ppermute | solution.py:402
  58.1 9.2 %collective-permute-start.10 = (f32[512,256]{1,0:T(8,128)S(1)}, f32[512,256]{1,0:T(8,128)S(1)}, u32[]{:S(2)}, u32[]{:S(2)}) collective-permute-start(f32[512,256]{1,0:T(8,128)S(1)} %get-tuple-element.101), channel_id=1, source_target_pairs={{4,8},{8,4},{12,16},{16,12},{20,24},{24,20},{5,9},{9,5},{13,17},{1... | collective-permute-start | bytes 1572872 | tf_op jit(solution)/shard_map/ppermute | solution.py:402
  58.8 8.5 %collective-permute-start.11 = (f32[512,256]{1,0:T(8,128)S(1)}, f32[512,256]{1,0:T(8,128)S(1)}, u32[]{:S(2)}, u32[]{:S(2)}) collective-permute-start(f32[512,256]{1,0:T(8,128)S(1)} %get-tuple-element.102), channel_id=1, source_target_pairs={{0,4},{4,0},{8,12},{12,8},{16,20},{20,16},{24,28},{28,24},{1,5},{5... | collective-permute-start | bytes 1572872 | tf_op jit(solution)/shard_map/ppermute | solution.py:402
  69.2 1.0 copy-start.3
  70.1 24.5 %all-to-all-start = ((f32[32,1,1536]{2,1,0:T(1,128)}), f32[32,1,1536]{2,1,0:T(1,128)S(1)}, u32[]{:S(2)}, u32[]{:S(2)}) async-start(f32[32,1,1536]{2,1,0:T(1,128)} %get-tuple-element.110), calls=%async_computation | async-start | bytes 393216 | tf_op jit(solution)/shard_map/all_to_all | solution.py:451
  94.7 1.2 %copy-start.4 = (f32[1024,256]{1,0:T(8,128)S(1)}, f32[1024,256]{1,0:T(8,128)}, u32[]{:S(2)}) copy-start(f32[1024,256]{1,0:T(8,128)} %copy-done.3) | copy-start | bytes 3145732

commit v2 on v0

v2 whole, which is shorter than its diff:
```python
import jax
import jax.numpy as jnp
from jax import lax
from jax.experimental import pallas as pl
from jax.experimental.pallas import tpu as pltpu
from jax.sharding import PartitionSpec as P


ITERS = 2
REACH = 2
EPS = 1e-06
CHUNKS = 2
LANES = 128
LIMIT = 12 * 2**20


def split(value):
    high = value.astype(jnp.bfloat16)
    low = (value - high.astype(jnp.float32)).astype(jnp.bfloat16)
    return high, low


def dot3(left_high, left_low, right_high, right_low):
    def dot(left, right):
        return jnp.dot(left, right, preferred_element_type=jnp.float32)

    return dot(left_high, right_high) + (dot(left_high, right_low) + dot(left_low, right_high))


def whole():
    return pl.BlockSpec(memory_space=pltpu.VMEM)


def scalar():
    return pl.BlockSpec(memory_space=pltpu.SMEM)


def call(kernel, out_shapes, in_specs, out_specs, flops, args, grid=(), scratch=(), aliases=None):
    return pl.pallas_call(
        kernel,
        grid=grid,
        in_specs=in_specs,
        out_specs=out_specs,
        out_shape=out_shapes,
        scratch_shapes=scratch,
        input_output_aliases=aliases or {},
        compiler_params=pltpu.CompilerParams(vmem_limit_bytes=LIMIT),
        cost_estimate=pl.CostEstimate(flops=flops, bytes_accessed=0, transcendentals=0),
    )(*args)


def f32(*shape):
    return jax.ShapeDtypeStruct(shape, jnp.float32)


def bf16(*shape):
    return jax.ShapeDtypeStruct(shape, jnp.bfloat16)


def in_hbm(value):
    return pltpu.with_memory_space_constraint(value, pltpu.HBM)


def store_sends(odd_ref, edge_ref, cross_ref, core_ref):
    half = edge_ref.shape[0] // 2
    first = odd_ref[0] * half
    first = pl.multiple_of(first, 256) if half % 256 == 0 else first
    second = half - first
    second = pl.multiple_of(second, 256) if half % 256 == 0 else second
    cross_ref[...] = edge_ref[pl.ds(first, half), :]
    core_ref[...] = edge_ref[pl.ds(second, half), :]


def prepare_kernel(value_ref, high_ref, low_ref):
    high, low = split(value_ref[...])
    high_ref[...] = high
    low_ref[...] = low


def prepare(value):
    count, rows, width = value.shape
    spec = pl.BlockSpec((1, rows, width), lambda i: (i, 0, 0))
    return call(
        prepare_kernel, (bf16(*value.shape), bf16(*value.shape)), [spec], (spec, spec),
        value.size, (value,), grid=(count,),
    )


def first_edges(right_side, precond, odd, across, chunk, width, after):
    nb, br, _ = precond.shape
    edge = REACH * br
    rows = nb * br

    def kernel(odd_ref, right_ref, matrix_ref, *refs):
        out_ref, value, matrix, arrived = refs[-4:]
        above = odd_ref[0] if across else 1 - odd_ref[0]
        here = pl.ds(pl.multiple_of(above * (rows - edge), edge), edge)
        copies = [
            pltpu.make_async_copy(right_ref.at[here, pl.ds(chunk * width, width)], value, arrived.at[0]),
            pltpu.make_async_copy(matrix_ref.at[pl.ds(above * (nb - REACH), REACH)], matrix, arrived.at[1]),
        ]
        for copy in copies:
            copy.start()
        for copy in copies:
            copy.wait()
        for j in range(REACH):
            data = split(value[j * br : (j + 1) * br, :])
            out_ref[j * br : (j + 1) * br, :] = dot3(*split(matrix[j]), *data)

    args = [odd, in_hbm(right_side), in_hbm(precond)]
    specs = [scalar()] + [pl.BlockSpec(memory_space=pltpu.HBM)] * 2
    if after is not None:
        args.append(after)
        specs.append(pl.BlockSpec(memory_space=pl.ANY))
    return call(
        kernel, f32(edge, width), specs, whole(), 6 * REACH * br * br * width, args,
        scratch=[
            pltpu.VMEM((edge, width), jnp.float32),
            pltpu.VMEM((REACH, br, br), jnp.float32),
            pltpu.SemaphoreType.DMA((2,)),
        ],
    )


def other_edges(right_side, precond, odd, width, after):
    nb, br, _ = precond.shape
    edge = REACH * br
    rows = nb * br
    todo = [(c, across) for c in range(CHUNKS) for across in (True, False)][1:]

    def kernel(odd_ref, right_ref, matrix_ref, _, *out_refs):
        for (c, across), out_ref in zip(todo, out_refs):
            above = odd_ref[0] if across else 1 - odd_ref[0]
            base = pl.multiple_of(above * (rows - edge), edge)
            for j in range(REACH):
                data = split(right_ref[pl.ds(base + j * br, br), c * width : (c + 1) * width])
                matrix = split(matrix_ref[above * (nb - REACH) + j])
                out_ref[j * br : (j + 1) * br, :] = dot3(*matrix, *data)

    return call(
        kernel, tuple(f32(edge, width) for _ in todo),
        [scalar(), whole(), whole(), pl.BlockSpec(memory_space=pl.ANY)], tuple(whole() for _ in todo),
        6 * REACH * len(todo) * br * br * width, [odd, right_side, precond, after],
    )


def bulk(residual, edge_step, total, band, precond, nb, br, width, chunk, after):
    first = total is None
    edge = REACH * br
    rows = nb * br
    inner = rows - 2 * edge
    reach = 2 * REACH + 1
    edge_rows = [*range(REACH), *range(nb - REACH, nb)]

    def at(j):
        return slice(j * br, (j + 1) * br)

    def kernel(*refs):
        refs = list(refs)
        if first:
            right_ref, odd_ref, cross_ref, core_ref = [refs.pop(0) for _ in range(4)]
        else:
            redge_ref, rinner_ref, dedge_ref, total_ref = [refs.pop(0) for _ in range(4)]
        ah_ref, al_ref, mh_ref, ml_ref, _, outedge_ref, outinner_ref, outtotal_ref = [refs.pop(0) for _ in range(8)]
        if not first:
            squares_ref = refs.pop(0)
        dh_ref, dl_ref = refs

        def load(j):
            if first:
                return right_ref[at(j), :]
            if j in edge_rows:
                return redge_ref[at(edge_rows.index(j)), :]
            return rinner_ref[at(j - REACH), :]

        def keep(j, d):
            high, low = split(d)
            dh_ref[at(j), :] = high
            dl_ref[at(j), :] = low
            outtotal_ref[at(j), :] = d if first else total_ref[at(j), :] + d

        if first:
            for ref, above in ((cross_ref, odd_ref[0]), (core_ref, 1 - odd_ref[0])):
                high, low = split(ref[...])
                here = pl.ds(pl.multiple_of(above * (rows - edge), edge), edge)
                dh_ref[here, :] = high
                dl_ref[here, :] = low
                outtotal_ref[here, :] = ref[...]
        else:
            for k, j in enumerate(edge_rows):
                keep(j, dedge_ref[at(k), :])
        for j in range(REACH, nb - REACH):
            keep(j, dot3(mh_ref[j], ml_ref[j], *split(load(j))))
        if not first:
            squares = jnp.zeros((8, width), jnp.float32)
            for j in range(nb):
                value = load(j)
                squares = squares + jnp.sum((value * value).reshape(-1, 8, width), axis=0)
            squares_ref[...] = jnp.sum(squares, axis=0, keepdims=True)
        for j in range(nb):
            start, stop = max(0, REACH - j), min(reach, nb + REACH - j)
            here = slice((j + start - REACH) * br, (j + stop - REACH) * br)
            columns = slice(start * br, stop * br)
            product = dot3(ah_ref[j, :, columns], al_ref[j, :, columns], dh_ref[here, :], dl_ref[here, :])
            if j in edge_rows:
                outedge_ref[at(edge_rows.index(j)), :] = load(j) - product
            else:
                outinner_ref[at(j - REACH), :] = load(j) - product

    specs = [pl.BlockSpec((rows, width), lambda i: (0, chunk)), scalar()] if first else [whole(), whole()]
    args = [*residual, *edge_step] + ([] if first else [total]) + [*band, *precond, after]
    specs += [whole()] * (len(args) - len(specs) - 1) + [pl.BlockSpec(memory_space=pl.ANY)]
    shapes = [f32(2 * edge, width), f32(inner, width), f32(rows, width)] + ([] if first else [f32(1, width)])
    products = (nb - 2 * REACH) + nb * reach - REACH * (REACH + 1)
    return call(
        kernel, tuple(shapes), specs, tuple(whole() for _ in shapes), 6 * products * br * br * width, args,
        grid=(1,), scratch=[pltpu.VMEM((rows, width), jnp.bfloat16), pltpu.VMEM((rows, width), jnp.bfloat16)],
    )


def halo_products(odd_ref, cross_ref, core_ref, ah_ref, al_ref, hh_ref, hl_ref, nb, br):
    edge = REACH * br
    odd_value = odd_ref[0]
    for ref, slot in ((cross_ref, odd_value), (core_ref, 1 - odd_value)):
        high, low = split(ref[...])
        here = pl.ds(pl.multiple_of(slot * edge, 8), edge)
        hh_ref[here, :] = high
        hl_ref[here, :] = low

    def product(k):
        if k < REACH:
            j, columns, here = k, slice(0, (REACH - k) * br), slice(k * br, edge)
        else:
            reached = k - REACH + 1
            j = k + nb - 2 * REACH
            columns = slice((2 * REACH + 1 - reached) * br, (2 * REACH + 1) * br)
            here = slice(edge, edge + reached * br)
        return dot3(ah_ref[j, :, columns], al_ref[j, :, columns], hh_ref[here, :], hl_ref[here, :])

    return product


def edges(partial_edge, cross, core, band, precond, odd, nb, br, width, after):
    edge = REACH * br

    def kernel(odd_ref, part_ref, cross_ref, core_ref, ah_ref, al_ref, mh_ref, ml_ref, _, *refs):
        out_ref, step_ref, sendx_ref, sends_ref, hh_ref, hl_ref = refs
        product = halo_products(odd_ref, cross_ref, core_ref, ah_ref, al_ref, hh_ref, hl_ref, nb, br)
        for k in range(2 * REACH):
            j = k if k < REACH else k + nb - 2 * REACH
            value = part_ref[k * br : (k + 1) * br, :] - product(k)
            out_ref[k * br : (k + 1) * br, :] = value
            step_ref[k * br : (k + 1) * br, :] = dot3(mh_ref[j], ml_ref[j], *split(value))
        store_sends(odd_ref, step_ref, sendx_ref, sends_ref)

    shapes = (f32(2 * edge, width), f32(2 * edge, width), f32(edge, width), f32(edge, width))
    args = [odd, partial_edge, cross, core, *band, *precond, after]
    specs = [scalar()] + [whole()] * (len(args) - 2) + [pl.BlockSpec(memory_space=pl.ANY)]
    return call(
        kernel, shapes, specs, tuple(whole() for _ in shapes),
        6 * (REACH * (REACH + 1) + 2 * REACH) * br * br * width, args,
        scratch=[pltpu.VMEM((2 * edge, width), jnp.bfloat16), pltpu.VMEM((2 * edge, width), jnp.bfloat16)],
    )


def edges_last(partial_edge, inner, cross, core, band, odd, nb, br, width, after, totals, earlier, devices):
    edge = REACH * br
    rows = nb * br
    answering = totals is not None

    def kernel(odd_ref, part_ref, inner_ref, cross_ref, core_ref, ah_ref, al_ref, *refs):
        refs = list(refs)
        copies = []
        if answering:
            total_refs = [refs.pop(0) for _ in range(CHUNKS)]
            _, out_ref, sums_ref, answer_ref, hh_ref, hl_ref, answered = refs
            for c in range(CHUNKS):
                there = answer_ref.at[:, pl.ds(c * width, width)]
                copies.append(pltpu.make_async_copy(total_refs[c], there, answered.at[c]))
                copies[-1].start()
        else:
            earlier_ref, _, out_ref, sums_ref, hh_ref, hl_ref = refs
        product = halo_products(odd_ref, cross_ref, core_ref, ah_ref, al_ref, hh_ref, hl_ref, nb, br)
        squares = jnp.zeros((8, width), jnp.float32)
        for k in range(2 * REACH):
            here = pl.ds(k * br, br)
            value = part_ref[here, :] - product(k)
            out_ref[here, :] = value
            squares = squares + jnp.sum((value * value).reshape(-1, 8, width), axis=0)
        for j in range(nb - 2 * REACH):
            value = inner_ref[j * br : (j + 1) * br, :]
            squares = squares + jnp.sum((value * value).reshape(-1, 8, width), axis=0)
        own = jnp.sum(squares, axis=0, keepdims=True)
        if answering:
            sums_ref[...] = own
        else:
            sums_ref[:, :, :width] = jnp.broadcast_to(own[None], (devices, 1, width))
            folded = earlier_ref[:, :LANES]
            for k in range(1, earlier_ref.shape[1] // LANES):
                folded = folded + earlier_ref[:, k * LANES : (k + 1) * LANES]
            sums_ref[:, :, width:] = jnp.broadcast_to(folded[None], (devices, 1, LANES))
        for copy in copies:
            copy.wait()

    args = [odd, partial_edge, inner, cross, core, *band]
    args += [*totals] if answering else [earlier]
    specs = [scalar()] + [whole()] * (len(args) - 1) + [pl.BlockSpec(memory_space=pl.ANY)]
    args.append(after)
    hbm = pl.BlockSpec(memory_space=pltpu.HBM)
    shapes = [f32(2 * edge, width)]
    shapes += [f32(1, width), pltpu.HBM((rows, CHUNKS * width), jnp.float32)] if answering else [f32(devices, 1, width + LANES)]
    outs = [whole(), whole()] + ([hbm] if answering else [])
    scratch = [
        pltpu.VMEM((2 * edge, width), jnp.bfloat16),
        pltpu.VMEM((2 * edge, width), jnp.bfloat16),
    ] + ([pltpu.SemaphoreType.DMA((CHUNKS,))] if answering else [])
    return call(
        kernel, tuple(shapes), specs, tuple(outs), 6 * REACH * (REACH + 1) * br * br * width, args,
        scratch=scratch,
    )


def scale_out(state, gathered, known, place, count, across, nb, br, width):
    rows = nb * br
    edge = REACH * br
    part = width // CHUNKS
    total_rows = count * rows

    def kernel(place_ref, *refs):
        pieces = refs[: 2 * CHUNKS]
        here_ref, known_ref, out_ref, history_ref, overall_ref, away, scaled, inverse, fetched, stored = refs[2 * CHUNKS :]
        fetch = pltpu.make_async_copy(pieces[1], away, fetched.at[0])
        fetch.start()
        place_value = place_ref[0]
        sums = [known_ref[:, k * part : (k + 1) * part] for k in range(known_ref.shape[1] // part)]
        value = here_ref[place_value, :, :part]
        for row in range(1, count):
            value = value + here_ref[place_value + row * across, :, :part]
        for k, value in enumerate(sums + [value]):
            sweep, c = divmod(k, CHUNKS)
            columns = slice(c * part, (c + 1) * part)
            root = jnp.sqrt(value / total_rows + EPS)
            history_ref[sweep : sweep + 1, columns] = root
            if sweep == ITERS:
                inverse[:, columns] = 1.0 / root
        copies = []
        jobs = [(c, 0, 0) for c in range(CHUNKS)] + [(c, 0, edge) for c in range(CHUNKS)]
        for c in list(range(1, CHUNKS)) + [0]:
            jobs += [(c, 1, start) for start in range(0, rows - 2 * edge, edge)]
        for number, (c, kind, start) in enumerate(jobs):
            if (c, kind, start) == (0, 1, 0):
                fetch.wait()
            ref = away if (c, kind) == (0, 1) else pieces[2 * c + kind]
            target = start + edge if kind else (rows - edge if start else 0)
            box = (pl.ds(target, edge), pl.ds(c * part, part))
            scaled[box] = ref[start : start + edge, :] * inverse[:, c * part : (c + 1) * part]
            copies.append(pltpu.make_async_copy(scaled.at[box], out_ref.at[box], stored.at[number]))
            copies[-1].start()
        total = jnp.sum(jnp.sum(here_ref[...], axis=0), axis=1, keepdims=True)
        overall_ref[...] = jnp.sqrt(total / (total_rows * across * width) + EPS)
        for copy in copies:
            copy.wait()

    args, specs = [place], [scalar()]
    hbm = pl.BlockSpec(memory_space=pltpu.HBM)
    for c, (outer, inner) in enumerate(state):
        args += [outer, inner if c else in_hbm(inner)]
        specs += [whole(), whole() if c else hbm]
    return call(
        kernel,
        (pltpu.HBM((rows, width), jnp.float32), f32(ITERS + 1, width), f32(1, 1)), specs + [whole(), whole()],
        (hbm, whole(), whole()), rows * width, args + [gathered, known],
        scratch=[
            pltpu.VMEM((rows - 2 * edge, part), jnp.float32),
            pltpu.VMEM((rows, width), jnp.float32),
            pltpu.VMEM((1, width), jnp.float32),
            pltpu.SemaphoreType.DMA((1,)),
            pltpu.SemaphoreType.DMA((CHUNKS * rows // edge,)),
        ],
    )


def swaps(count):
    core = [(i, i ^ 1) for i in range(count) if (i ^ 1) < count]
    cross = []
    for i in range(1, count - 1, 2):
        cross += [(i, i + 1), (i + 1, i)]
    return core, cross


def shards(band_blocks, precond_blocks, right_side):
    nb, br, _ = precond_blocks.shape
    width = right_side.shape[1]
    part = width // CHUNKS
    count = lax.axis_size("rows")
    across = lax.axis_size("rhs")
    core_pairs, cross_pairs = swaps(count)
    odd = (lax.axis_index("rows") % 2).astype(jnp.int32)[None]

    def exchange(cross_send, core_send):
        cross = lax.ppermute(cross_send, "rows", cross_pairs)
        return cross, lax.ppermute(core_send, "rows", core_pairs)

    place = lax.axis_index("rhs").astype(jnp.int32)[None]
    step, halo = [], []
    after = first_edges(right_side, precond_blocks, odd, True, 0, part, None)
    sends = [after, *other_edges(right_side, precond_blocks, odd, part, after)]
    after = sends[-1]
    for c in range(CHUNKS):
        step.append(sends[2 * c : 2 * c + 2])
        halo.append(exchange(*step[c]))
    band = prepare(band_blocks)
    precond = prepare(precond_blocks)
    outer, inner, total = [None] * CHUNKS, [None] * CHUNKS, [None] * CHUNKS
    sums = [[None] * CHUNKS for _ in range(ITERS)]
    latest = [after]

    def run_bulk(sweep, c):
        if sweep < 0:
            residual, edge_step = (right_side,), (odd, *step[c])
        else:
            residual, edge_step = (outer[c], inner[c]), (step[c],)
        done = bulk(residual, edge_step, total[c], band, precond, nb, br, part, c, latest[0])
        outer[c], inner[c], total[c] = done[:3]
        if sweep >= 0:
            sums[sweep][c] = done[3]
        latest[0] = outer[c]

    def run_edges(c):
        outer[c], step[c], cross_send, core_send = edges(
            outer[c], *halo[c], band, precond, odd, nb, br, part, latest[0]
        )
        halo[c] = exchange(cross_send, core_send)
        latest[0] = outer[c]

    for sweep in range(ITERS):
        for c in range(CHUNKS):
            run_bulk(sweep - 1, c)
            run_edges(c)
    for c in range(CHUNKS):
        run_bulk(ITERS - 1, c)
    known = [value for row in sums for value in row]
    local = []
    for c in range(CHUNKS):
        final = c == CHUNKS - 1
        if final:
            known = jnp.concatenate(known + local, axis=1)
            hops = [1 << k for k in range((count - 1).bit_length())]
            for hop in hops[:1] + hops[2:] + hops[1:2]:
                latest[0] = known
                known = known + lax.ppermute(known, "rows", [(i, i ^ hop) for i in range(count)])
        done = edges_last(
            outer[c], inner[c], *halo[c], band, odd, nb, br, part, latest[0],
            None if final else total, jnp.concatenate(local, axis=1) if final else None, count * across,
        )
        outer[c], latest[0] = done[0], done[1]
        if final:
            message = done[1]
        else:
            local.append(done[1])
            answer = done[2]
    gathered = lax.all_to_all(message, ("rows", "rhs"), 0, 0, tiled=True)
    scaled, history, overall = scale_out(
        list(zip(outer, inner)), gathered, known, place, count, across, nb, br, width
    )
    return (answer, scaled, history, overall.reshape(()))


def solution(mesh):
    in_specs = (P("rows", None, None), P("rows", None, None), P("rows", "rhs"))
    out_specs = (P("rows", "rhs"), P("rows", "rhs"), P(None, "rhs"), P())

    return jax.shard_map(shards, mesh=mesh, in_specs=in_specs, out_specs=out_specs, check_vma=False)
```

time: 225 us -> 95.4 us (0.42)
  the two profiles are of different devices: /device:TPU:4 before, /device:TPU:0 now
where the time goes in v2:
time: 95.4 us; the launch traced here: 95 us
  Pallas kernels  47.4 us (50%)
  starting transfers between devices  33.1 us (35%)
  waiting for transfers between devices  8.74 us (9%)
  local copies, waits for them, and re-layouts  4.57 us (5%)
  between operations  1.17 us (1%)
    pallas_call x17, Pallas kernels, call(): pl.pallas_call(kernel, grid=grid, in_specs=in_specs, out_specs=out_specs,...  47.4 us
    ppermute x6, starting transfers between devices, exchange(): return (cross, lax.ppermute(core_send, 'rows', core_pairs))  18.4 us
    all_to_all x1, starting transfers between devices, shards(): gathered = lax.all_to_all(message, ('rows', 'rhs'), 0, 0, tiled=True)  6.42 us
    ppermute x3, waiting for transfers between devices, shards(): lax.ppermute(known, 'rows', [(i, i ^ hop) for i in range(count)])  5 us
    ppermute x6, starting transfers between devices, exchange(): cross = lax.ppermute(cross_send, 'rows', cross_pairs)  4.69 us
    unnamed x12, local copies, waits for them, and re-layouts  4.56 us
    all_to_all x1, waiting for transfers between devices, shards(): gathered = lax.all_to_all(message, ('rows', 'rhs'), 0, 0, tiled=True)  3.71 us
    ppermute x3, starting transfers between devices, shards(): lax.ppermute(known, 'rows', [(i, i ^ hop) for i in range(count)])  3.59 us
  transfers between devices with their start and end apart: 16, of which 4 were waited for; matrix products, arithmetic and copies ran while one was open for 0% of the time, Pallas kernels for 42%

profile of v2, /device:TPU:0, one launch (start us, length us, event | category | flops | bytes accessed | tf_op | source)
XLA Modules:
  0.0 95.0 jit_solution(5093003042672258644)
XLA Ops:
  4.7 3.8 %collective-permute-start.1 = (f32[512,256]{1,0:T(8,128)S(1)}, f32[512,256]{1,0:T(8,128)S(1)}, u32[]{:S(2)}, u32[]{:S(2)}) collective-permute-start(f32[512,256]{1,0:T(8,128)S(1)} %get-tuple-element.57.refs_3_), channel_id=1, source_target_pairs={{0,4},{4,0},{8,12},{12,8},{16,20},{20,16},{24,28},{28,24},{1,5},{5... | collective-permute-start | bytes 1572872 | tf_op jit(solution)/shard_map/ppermute | solution.py:402
  9.2 2.9 %collective-permute-start.3 = (f32[512,256]{1,0:T(8,128)S(1)}, f32[512,256]{1,0:T(8,128)S(1)}, u32[]{:S(2)}, u32[]{:S(2)}) collective-permute-start(f32[512,256]{1,0:T(8,128)S(1)} %get-tuple-element.62.refs_8_.refs_3_), channel_id=1, source_target_pairs={{0,4},{4,0},{8,12},{12,8},{16,20},{20,16},{24,28},{28,24},{1,5},{5... | collective-permute-start | bytes 1572872 | tf_op jit(solution)/shard_map/ppermute | solution.py:402
  12.5 4.0 %copy-done.2 = f32[8,256,1280]{2,1,0:T(8,128)S(1)} copy-done((f32[8,256,1280]{2,1,0:T(8,128)S(1)}, f32[8,256,1280]{2,1,0:T(8,128)}, u32[]{:S(2)}) %copy-start.2) | copy-done | bytes 10485784
  18.0 4.5 %shard_map.70 = (f32[1024,256]{1,0:T(8,128)S(1)}, f32[1024,256]{1,0:T(8,128)S(1)}, f32[2048,256]{1,0:T(8,128)S(1)}) custom-call(f32[2048,512]{1,0:T(8,128)S(1)} %copy-done, s32[1]{0:T(128)} %bitcast.odd_ref.refs_1_, f32[512,256]{1,0:T(8,128)S(1)} %shard_map.66._.refs_2_, f32[512,256]{1,0:T(8,128)S(1)} %get-tuple-element.57.refs_3_, ...), custom_call_target="tpu_custom_call" | custom-call | flops 3825205248 | tf_op jit(solution)/shard_map/pallas_call | solution.py:39
  22.6 2.3 %shard_map.71 = (f32[1024,256]{1,0:T(8,128)S(1)}, f32[1024,256]{1,0:T(8,128)S(1)}, f32[512,256]{1,0:T(8,128)S(1)}, f32[512,256]{1,0:T(8,128)S(1)}) custom-call(s32[1]{0:T(128)} %bitcast.odd_ref.refs_1_, f32[1024,256]{1,0:T(8,128)S(1)} %get-tuple-element.63.part_ref._, f32[512,256]{1,0:T(8,128)S(1)} %collective-permute-done.cross_ref, ...), custom_call_target="tpu_custom_call" | custom-call | flops 1006632960 | tf_op jit(solution)/shard_map/pallas_call | solution.py:39
  25.7 2.9 %collective-permute-start.5 = (f32[512,256]{1,0:T(8,128)S(1)}, f32[512,256]{1,0:T(8,128)S(1)}, u32[]{:S(2)}, u32[]{:S(2)}) collective-permute-start(f32[512,256]{1,0:T(8,128)S(1)} %get-tuple-element.73), channel_id=1, source_target_pairs={{0,4},{4,0},{8,12},{12,8},{16,20},{20,16},{24,28},{28,24},{1,5},{5... | collective-permute-start | bytes 1572872 | tf_op jit(solution)/shard_map/ppermute | solution.py:402
  28.6 4.5 %shard_map.72 = (f32[1024,256]{1,0:T(8,128)S(1)}, f32[1024,256]{1,0:T(8,128)S(1)}, f32[2048,256]{1,0:T(8,128)S(1)}) custom-call(f32[2048,512]{1,0:T(8,128)S(1)} %copy-done, s32[1]{0:T(128)} %bitcast.odd_ref.refs_1_, f32[512,256]{1,0:T(8,128)S(1)} %get-tuple-element.68.refs_2_, f32[512,256]{1,0:T(8,128)S(1)} %get-tuple-element.62.refs_8_.refs_3_, ...), custom_call_target="tpu_custom_call" | custom-call | flops 3825205248 | tf_op jit(solution)/shard_map/pallas_call | solution.py:39
  33.2 2.3 %shard_map.73 = (f32[1024,256]{1,0:T(8,128)S(1)}, f32[1024,256]{1,0:T(8,128)S(1)}, f32[512,256]{1,0:T(8,128)S(1)}, f32[512,256]{1,0:T(8,128)S(1)}) custom-call(s32[1]{0:T(128)} %bitcast.odd_ref.refs_1_, f32[1024,256]{1,0:T(8,128)S(1)} %get-tuple-element.69.part_ref._, f32[512,256]{1,0:T(8,128)S(1)} %collective-permute-done.2.cross_ref, ...), custom_call_target="tpu_custom_call" | custom-call | flops 1006632960 | tf_op jit(solution)/shard_map/pallas_call | solution.py:39
  36.2 2.4 %collective-permute-start.7 = (f32[512,256]{1,0:T(8,128)S(1)}, f32[512,256]{1,0:T(8,128)S(1)}, u32[]{:S(2)}, u32[]{:S(2)}) collective-permute-start(f32[512,256]{1,0:T(8,128)S(1)} %get-tuple-element.83), channel_id=1, source_target_pairs={{0,4},{4,0},{8,12},{12,8},{16,20},{20,16},{24,28},{28,24},{1,5},{5... | collective-permute-start | bytes 1572872 | tf_op jit(solution)/shard_map/ppermute | solution.py:402
  38.5 4.3 %shard_map.74 = (f32[1024,256]{1,0:T(8,128)S(1)}, f32[1024,256]{1,0:T(8,128)S(1)}, f32[2048,256]{1,0:T(8,128)S(1)}, f32[1,256]{1,0:T(1,128)S(1)}) custom-call(f32[1024,256]{1,0:T(8,128)S(1)} %get-tuple-element.64.refs_8_.refs_0_, f32[1024,256]{1,0:T(8,128)S(1)} %get-tuple-element.65.refs_1_, f32[1024,256]{1,0:T(8,128)S(1)} %get-tuple-element.66.refs_2_, ...), custom_call_target="tpu_custom_call" | custom-call | flops 3825205248 | tf_op jit(solution)/shard_map/pallas_call | solution.py:39
  42.9 2.3 %shard_map.75 = (f32[1024,256]{1,0:T(8,128)S(1)}, f32[1024,256]{1,0:T(8,128)S(1)}, f32[512,256]{1,0:T(8,128)S(1)}, f32[512,256]{1,0:T(8,128)S(1)}) custom-call(s32[1]{0:T(128)} %bitcast.odd_ref.refs_1_, f32[1024,256]{1,0:T(8,128)S(1)} %get-tuple-element.71.part_ref._, f32[512,256]{1,0:T(8,128)S(1)} %collective-permute-done.4.cross_ref, ...), custom_call_target="tpu_custom_call" | custom-call | flops 1006632960 | tf_op jit(solution)/shard_map/pallas_call | solution.py:39
  46.1 2.9 %collective-permute-start.9 = (f32[512,256]{1,0:T(8,128)S(1)}, f32[512,256]{1,0:T(8,128)S(1)}, u32[]{:S(2)}, u32[]{:S(2)}) collective-permute-start(f32[512,256]{1,0:T(8,128)S(1)} %get-tuple-element.88), channel_id=1, source_target_pairs={{0,4},{4,0},{8,12},{12,8},{16,20},{20,16},{24,28},{28,24},{1,5},{5... | collective-permute-start | bytes 1572872 | tf_op jit(solution)/shard_map/ppermute | solution.py:402
  49.0 4.3 %shard_map.76 = (f32[1024,256]{1,0:T(8,128)S(1)}, f32[1024,256]{1,0:T(8,128)S(1)}, f32[2048,256]{1,0:T(8,128)S(1)}, f32[1,256]{1,0:T(1,128)S(1)}) custom-call(f32[1024,256]{1,0:T(8,128)S(1)} %get-tuple-element.70.refs_8_.refs_0_, f32[1024,256]{1,0:T(8,128)S(1)} %get-tuple-element.78.refs_1_, f32[1024,256]{1,0:T(8,128)S(1)} %get-tuple-element.79.refs_2_, ...), custom_call_target="tpu_custom_call" | custom-call | flops 3825205248 | tf_op jit(solution)/shard_map/pallas_call | solution.py:39
  53.3 2.3 %shard_map.77 = (f32[1024,256]{1,0:T(8,128)S(1)}, f32[1024,256]{1,0:T(8,128)S(1)}, f32[512,256]{1,0:T(8,128)S(1)}, f32[512,256]{1,0:T(8,128)S(1)}) custom-call(s32[1]{0:T(128)} %bitcast.odd_ref.refs_1_, f32[1024,256]{1,0:T(8,128)S(1)} %get-tuple-element.81.part_ref._, f32[512,256]{1,0:T(8,128)S(1)} %collective-permute-done.6.cross_ref, ...), custom_call_target="tpu_custom_call" | custom-call | flops 1006632960 | tf_op jit(solution)/shard_map/pallas_call | solution.py:39
  56.3 3.5 %collective-permute-start.11 = (f32[512,256]{1,0:T(8,128)S(1)}, f32[512,256]{1,0:T(8,128)S(1)}, u32[]{:S(2)}, u32[]{:S(2)}) collective-permute-start(f32[512,256]{1,0:T(8,128)S(1)} %get-tuple-element.99), channel_id=1, source_target_pairs={{0,4},{4,0},{8,12},{12,8},{16,20},{20,16},{24,28},{28,24},{1,5},{5... | collective-permute-start | bytes 1572872 | tf_op jit(solution)/shard_map/ppermute | solution.py:402
  59.9 4.3 %shard_map.78 = (f32[1024,256]{1,0:T(8,128)S(1)}, f32[1024,256]{1,0:T(8,128)S(1)}, f32[2048,256]{1,0:T(8,128)S(1)}, f32[1,256]{1,0:T(1,128)S(1)}) custom-call(f32[1024,256]{1,0:T(8,128)S(1)} %get-tuple-element.74.refs_8_.refs_0_, f32[1024,256]{1,0:T(8,128)S(1)} %get-tuple-element.75.refs_1_, f32[1024,256]{1,0:T(8,128)S(1)} %get-tuple-element.76.refs_2_, ...), custom_call_target="tpu_custom_call" | custom-call | flops 3825205248 | tf_op jit(solution)/shard_map/pallas_call | solution.py:39
  64.2 4.3 %shard_map.79 = (f32[1024,256]{1,0:T(8,128)S(1)}, f32[1024,256]{1,0:T(8,128)S(1)}, f32[2048,256]{1,0:T(8,128)S(1)}, f32[1,256]{1,0:T(1,128)S(1)}) custom-call(f32[1024,256]{1,0:T(8,128)S(1)} %get-tuple-element.84.refs_8_.refs_0_, f32[1024,256]{1,0:T(8,128)S(1)} %get-tuple-element.90.refs_1_, f32[1024,256]{1,0:T(8,128)S(1)} %get-tuple-element.91.refs_2_, ...), custom_call_target="tpu_custom_call" | custom-call | flops 3825205248 | tf_op jit(solution)/shard_map/pallas_call | solution.py:39
  68.7 2.1 %shard_map.80 = (f32[1024,256]{1,0:T(8,128)S(1)}, f32[1,256]{1,0:T(1,128)S(1)}, f32[2048,512]{1,0:T(8,128)}) custom-call(s32[1]{0:T(128)} %bitcast.odd_ref.refs_1_, f32[1024,256]{1,0:T(8,128)S(1)} %get-tuple-element.85.refs_8_.part_ref, f32[1024,256]{1,0:T(8,128)S(1)} %get-tuple-element.86.inner_ref.refs_1_, ...), custom_call_target="tpu_custom_call" | custom-call | flops 603979776 | tf_op jit(solution)/shard_map/pallas_call | solution.py:39
  73.7 2.0 %collective-permute-done.13 = f32[1,1280]{1,0:T(1,128)S(1)} collective-permute-done((f32[1,1280]{1,0:T(1,128)S(1)}, f32[1,1280]{1,0:T(1,128)S(1)}, u32[]{:S(2)}, u32[]{:S(2)}) %collective-permute-start.13) | collective-permute-done | bytes 5152 | tf_op jit(solution)/shard_map/ppermute | solution.py:451
  77.4 6.4 %all-to-all-start = ((f32[32,1,384]{2,1,0:T(1,128)}), f32[32,1,384]{2,1,0:T(1,128)S(1)}, u32[]{:S(2)}, u32[]{:S(2)}) async-start(f32[32,1,384]{2,1,0:T(1,128)} %get-tuple-element.106), calls=%async_computation | async-start | bytes 98304 | tf_op jit(solution)/shard_map/all_to_all | solution.py:462
  83.9 1.8 %collective-permute-start.14 = (f32[1,1280]{1,0:T(1,128)S(1)}, f32[1,1280]{1,0:T(1,128)S(1)}, u32[]{:S(2)}, u32[]{:S(2)}) collective-permute-start(f32[1,1280]{1,0:T(1,128)S(1)} %add.15.refs_1_), channel_id=1, source_target_pairs={{0,8},{4,12},{8,0},{12,4},{16,24},{20,28},{24,16},{28,20},{1,9},{5... | collective-permute-start | bytes 15368 | tf_op jit(solution)/shard_map/ppermute | solution.py:451
  85.7 1.9 %collective-permute-done.14 = f32[1,1280]{1,0:T(1,128)S(1)} collective-permute-done((f32[1,1280]{1,0:T(1,128)S(1)}, f32[1,1280]{1,0:T(1,128)S(1)}, u32[]{:S(2)}, u32[]{:S(2)}) %collective-permute-start.14) | collective-permute-done | bytes 5152 | tf_op jit(solution)/shard_map/ppermute | solution.py:451
  87.6 3.7 %all-to-all-done.refs_4_ = f32[32,1,384]{2,1,0:T(1,128)S(1)} async-done(((f32[32,1,384]{2,1,0:T(1,128)}), f32[32,1,384]{2,1,0:T(1,128)S(1)}, u32[]{:S(2)}, u32[]{:S(2)}) %all-to-all-start) | async-done | bytes 49184 | tf_op jit(solution)/shard_map/all_to_all | solution.py:462
  91.3 3.5 %shard_map.82 = (f32[2048,512]{1,0:T(8,128)}, f32[3,512]{1,0:T(4,128)}, f32[1,1]{1,0:T(1,128)}) custom-call(s32[1]{0:T(128)} %bitcast.1.place_ref, f32[1024,256]{1,0:T(8,128)S(1)} %get-tuple-element.96.refs_0_, f32[1024,256]{1,0:T(8,128)} %copy-done.3, f32[1024,256]{1,0:T(8,128)S(1)} %get-tuple-element.105.refs_2_, ...), custom_call_target="tpu_custom_call" | custom-call | flops 1048576 | tf_op jit(solution)/shard_map/pallas_call | solution.py:39
  (41 shorter events, 14.5 us)
Async XLA Ops:
  0.6 2.6 %copy-start = (f32[2048,512]{1,0:T(8,128)S(1)}, f32[2048,512]{1,0:T(8,128)}, u32[]{:S(2)}) copy-start(f32[2048,512]{1,0:T(8,128)} %refs_0_.3) | copy-start | bytes 12582916
  0.7 3.2 %copy-start.1 = (f32[8,256,256]{2,1,0:T(8,128)S(1)}, f32[8,256,256]{2,1,0:T(8,128)}, u32[]{:S(2)}) copy-start(f32[8,256,256]{2,1,0:T(8,128)} %value_ref.3) | copy-start | bytes 6291460
  2.4 20.1 %collective-permute-start = (f32[512,256]{1,0:T(8,128)S(1)}, f32[512,256]{1,0:T(8,128)S(1)}, u32[]{:S(2)}, u32[]{:S(2)}) collective-permute-start(f32[512,256]{1,0:T(8,128)S(1)} %shard_map.66._.refs_2_), channel_id=1, source_target_pairs={{4,8},{8,4},{12,16},{16,12},{20,24},{24,20},{5,9},{9,5},{13,17},{1... | collective-permute-start | bytes 1572872 | tf_op jit(solution)/shard_map/ppermute | solution.py:401
  4.7 17.9 %collective-permute-start.1 = (f32[512,256]{1,0:T(8,128)S(1)}, f32[512,256]{1,0:T(8,128)S(1)}, u32[]{:S(2)}, u32[]{:S(2)}) collective-permute-start(f32[512,256]{1,0:T(8,128)S(1)} %get-tuple-element.57.refs_3_), channel_id=1, source_target_pairs={{0,4},{4,0},{8,12},{12,8},{16,20},{20,16},{24,28},{28,24},{1,5},{5... | collective-permute-start | bytes 1572872 | tf_op jit(solution)/shard_map/ppermute | solution.py:402
  8.5 24.6 %collective-permute-start.2 = (f32[512,256]{1,0:T(8,128)S(1)}, f32[512,256]{1,0:T(8,128)S(1)}, u32[]{:S(2)}, u32[]{:S(2)}) collective-permute-start(f32[512,256]{1,0:T(8,128)S(1)} %get-tuple-element.68.refs_2_), channel_id=1, source_target_pairs={{4,8},{8,4},{12,16},{16,12},{20,24},{24,20},{5,9},{9,5},{13,17},{1... | collective-permute-start | bytes 1572872 | tf_op jit(solution)/shard_map/ppermute | solution.py:401
  9.2 23.9 %collective-permute-start.3 = (f32[512,256]{1,0:T(8,128)S(1)}, f32[512,256]{1,0:T(8,128)S(1)}, u32[]{:S(2)}, u32[]{:S(2)}) collective-permute-start(f32[512,256]{1,0:T(8,128)S(1)} %get-tuple-element.62.refs_8_.refs_3_), channel_id=1, source_target_pairs={{0,4},{4,0},{8,12},{12,8},{16,20},{20,16},{24,28},{28,24},{1,5},{5... | collective-permute-start | bytes 1572872 | tf_op jit(solution)/shard_map/ppermute | solution.py:402
  12.5 4.0 %copy-start.2 = (f32[8,256,1280]{2,1,0:T(8,128)S(1)}, f32[8,256,1280]{2,1,0:T(8,128)}, u32[]{:S(2)}) copy-start(f32[8,256,1280]{2,1,0:T(8,128)} %value_ref.2) | copy-start | bytes 31457284
  24.9 18.0 %collective-permute-start.4 = (f32[512,256]{1,0:T(8,128)S(1)}, f32[512,256]{1,0:T(8,128)S(1)}, u32[]{:S(2)}, u32[]{:S(2)}) collective-permute-start(f32[512,256]{1,0:T(8,128)S(1)} %get-tuple-element.72), channel_id=1, source_target_pairs={{4,8},{8,4},{12,16},{16,12},{20,24},{24,20},{5,9},{9,5},{13,17},{1... | collective-permute-start | bytes 1572872 | tf_op jit(solution)/shard_map/ppermute | solution.py:401
  25.7 17.1 %collective-permute-start.5 = (f32[512,256]{1,0:T(8,128)S(1)}, f32[512,256]{1,0:T(8,128)S(1)}, u32[]{:S(2)}, u32[]{:S(2)}) collective-permute-start(f32[512,256]{1,0:T(8,128)S(1)} %get-tuple-element.73), channel_id=1, source_target_pairs={{0,4},{4,0},{8,12},{12,8},{16,20},{20,16},{24,28},{28,24},{1,5},{5... | collective-permute-start | bytes 1572872 | tf_op jit(solution)/shard_map/ppermute | solution.py:402
  35.5 17.9 %collective-permute-start.6 = (f32[512,256]{1,0:T(8,128)S(1)}, f32[512,256]{1,0:T(8,128)S(1)}, u32[]{:S(2)}, u32[]{:S(2)}) collective-permute-start(f32[512,256]{1,0:T(8,128)S(1)} %get-tuple-element.82), channel_id=1, source_target_pairs={{4,8},{8,4},{12,16},{16,12},{20,24},{24,20},{5,9},{9,5},{13,17},{1... | collective-permute-start | bytes 1572872 | tf_op jit(solution)/shard_map/ppermute | solution.py:401
  36.2 17.2 %collective-permute-start.7 = (f32[512,256]{1,0:T(8,128)S(1)}, f32[512,256]{1,0:T(8,128)S(1)}, u32[]{:S(2)}, u32[]{:S(2)}) collective-permute-start(f32[512,256]{1,0:T(8,128)S(1)} %get-tuple-element.83), channel_id=1, source_target_pairs={{0,4},{4,0},{8,12},{12,8},{16,20},{20,16},{24,28},{28,24},{1,5},{5... | collective-permute-start | bytes 1572872 | tf_op jit(solution)/shard_map/ppermute | solution.py:402
  45.2 23.5 %collective-permute-start.8 = (f32[512,256]{1,0:T(8,128)S(1)}, f32[512,256]{1,0:T(8,128)S(1)}, u32[]{:S(2)}, u32[]{:S(2)}) collective-permute-start(f32[512,256]{1,0:T(8,128)S(1)} %get-tuple-element.87), channel_id=1, source_target_pairs={{4,8},{8,4},{12,16},{16,12},{20,24},{24,20},{5,9},{9,5},{13,17},{1... | collective-permute-start | bytes 1572872 | tf_op jit(solution)/shard_map/ppermute | solution.py:401
  46.1 22.6 %collective-permute-start.9 = (f32[512,256]{1,0:T(8,128)S(1)}, f32[512,256]{1,0:T(8,128)S(1)}, u32[]{:S(2)}, u32[]{:S(2)}) collective-permute-start(f32[512,256]{1,0:T(8,128)S(1)} %get-tuple-element.88), channel_id=1, source_target_pairs={{0,4},{4,0},{8,12},{12,8},{16,20},{20,16},{24,28},{28,24},{1,5},{5... | collective-permute-start | bytes 1572872 | tf_op jit(solution)/shard_map/ppermute | solution.py:402
  55.6 20.1 %collective-permute-start.10 = (f32[512,256]{1,0:T(8,128)S(1)}, f32[512,256]{1,0:T(8,128)S(1)}, u32[]{:S(2)}, u32[]{:S(2)}) collective-permute-start(f32[512,256]{1,0:T(8,128)S(1)} %get-tuple-element.98), channel_id=1, source_target_pairs={{4,8},{8,4},{12,16},{16,12},{20,24},{24,20},{5,9},{9,5},{13,17},{1... | collective-permute-start | bytes 1572872 | tf_op jit(solution)/shard_map/ppermute | solution.py:401
  56.3 19.4 %collective-permute-start.11 = (f32[512,256]{1,0:T(8,128)S(1)}, f32[512,256]{1,0:T(8,128)S(1)}, u32[]{:S(2)}, u32[]{:S(2)}) collective-permute-start(f32[512,256]{1,0:T(8,128)S(1)} %get-tuple-element.99), channel_id=1, source_target_pairs={{0,4},{4,0},{8,12},{12,8},{16,20},{20,16},{24,28},{28,24},{1,5},{5... | collective-permute-start | bytes 1572872 | tf_op jit(solution)/shard_map/ppermute | solution.py:402
  64.2 4.4 %copy-start.3 = (f32[1024,256]{1,0:T(8,128)}, f32[1024,256]{1,0:T(8,128)S(1)}, u32[]{:S(2)}) copy-start(f32[1024,256]{1,0:T(8,128)S(1)} %get-tuple-element.86.inner_ref.refs_1_) | copy-start | bytes 3145732
  70.8 1.2 %collective-permute-start.12 = (f32[1,1280]{1,0:T(1,128)S(1)}, f32[1,1280]{1,0:T(1,128)S(1)}, u32[]{:S(2)}, u32[]{:S(2)}) collective-permute-start(f32[1,1280]{1,0:T(1,128)S(1)} %constant_dynamic-update-slice_fusion), channel_id=1, source_target_pairs={{0,4},{4,0},{8,12},{12,8},{16,20},{20,16},{24,28},{28,24},{1,5},{5... | collective-permute-start | bytes 15368 | tf_op jit(solution)/shard_map/ppermute | solution.py:451
  72.0 3.7 %collective-permute-start.13 = (f32[1,1280]{1,0:T(1,128)S(1)}, f32[1,1280]{1,0:T(1,128)S(1)}, u32[]{:S(2)}, u32[]{:S(2)}) collective-permute-start(f32[1,1280]{1,0:T(1,128)S(1)} %add.14), channel_id=1, source_target_pairs={{0,16},{4,20},{8,24},{12,28},{16,0},{20,4},{24,8},{28,12},{1,17},{... | collective-permute-start | bytes 15368 | tf_op jit(solution)/shard_map/ppermute | solution.py:451
  77.4 13.8 %all-to-all-start = ((f32[32,1,384]{2,1,0:T(1,128)}), f32[32,1,384]{2,1,0:T(1,128)S(1)}, u32[]{:S(2)}, u32[]{:S(2)}) async-start(f32[32,1,384]{2,1,0:T(1,128)} %get-tuple-element.106), calls=%async_computation | async-start | bytes 98304 | tf_op jit(solution)/shard_map/all_to_all | solution.py:462
  83.9 3.7 %collective-permute-start.14 = (f32[1,1280]{1,0:T(1,128)S(1)}, f32[1,1280]{1,0:T(1,128)S(1)}, u32[]{:S(2)}, u32[]{:S(2)}) collective-permute-start(f32[1,1280]{1,0:T(1,128)S(1)} %add.15.refs_1_), channel_id=1, source_target_pairs={{0,8},{4,12},{8,0},{12,4},{16,24},{20,28},{24,16},{28,20},{1,9},{5... | collective-permute-start | bytes 15368 | tf_op jit(solution)/shard_map/ppermute | solution.py:451
